TPU v7x, 8 devices: a whole 2x2x1 slice. The times are simulated.
8 devices in a mesh: rep: 1 (over z), fsdp: 8 (over y, x, core).
Axes of the slice: x: 2, y: 2, z: 1, core: 2. Of those that a mesh axis runs over, the one named last changes fastest.
Arguments:
- tokens: bfloat16 [8192, 1536], P(('rep', 'fsdp'))
- seg_ids: int32 [8192], P(('rep', 'fsdp'))
- w_q: bfloat16 [2, 1536, 1536], P(None, 'fsdp')
- w_k: bfloat16 [2, 1536, 256], P(None, 'fsdp')
- w_v: bfloat16 [2, 1536, 256], P(None, 'fsdp')
- w_o: bfloat16 [2, 1536, 1536], P(None, 'fsdp')
- w_gate: bfloat16 [2, 1536, 8960], P(None, 'fsdp')
- w_up: bfloat16 [2, 1536, 8960], P(None, 'fsdp')
- w_down: bfloat16 [2, 8960, 1536], P(None, 'fsdp')
- g_attn: bfloat16 [2, 1536], replicated
- g_mlp: bfloat16 [2, 1536], replicated
Outputs:
- output: float32 [8192, 1536], P(('rep', 'fsdp'))
All inputs are finite; a program needn't handle non-finite values.
Results may differ from a plain program's by a relative error of at most 0.0138107.
Values are sent between devices in bfloat16 or wider.
A program may use at most 1 GiB of HBM per device.

v0:
```python
import jax
import jax.numpy as jnp
from jax import lax
from jax.sharding import PartitionSpec as P

HEAD = 128
EPS = 1e-5
ROPE_BASE = 10000.0


def rms_norm(hidden, gain):
    inv_rms = lax.rsqrt(jnp.mean(hidden * hidden, axis=-1, keepdims=True) + EPS)
    return (hidden * inv_rms * gain.astype(jnp.float32)).astype(jnp.bfloat16)


def rope_tables(seg_blk):
    tok_idx = lax.broadcasted_iota(jnp.int32, seg_blk.shape, 1)
    is_first = jnp.concatenate([tok_idx[:, :1] == 0, seg_blk[:, 1:] != seg_blk[:, :-1]], axis=1)
    req_start = lax.cummax(jnp.where(is_first, tok_idx, 0), axis=1)
    tok_pos = (tok_idx - req_start).astype(jnp.float32)
    half_dim = HEAD // 2
    inv_freq = ROPE_BASE ** (-jnp.arange(half_dim, dtype=jnp.float32) / half_dim)
    angles = tok_pos[:, :, None] * inv_freq
    return jnp.cos(angles), jnp.sin(angles)


def attention_mask(seg_blk):
    tok_idx = jnp.arange(seg_blk.shape[1], dtype=jnp.int32)
    causal = tok_idx[:, None] >= tok_idx[None, :]
    same_req = seg_blk[:, :, None] == seg_blk[:, None, :]
    return (same_req & causal)[:, None, None]


def apply_rope(vals, cos_tab, sin_tab):
    half_dim = HEAD // 2
    bcast_shape = cos_tab.shape[:2] + (1,) * (vals.ndim - 3) + (half_dim,)
    cos_wide = cos_tab.reshape(bcast_shape)
    sin_wide = sin_tab.reshape(bcast_shape)
    first_half = vals[..., :half_dim].astype(jnp.float32)
    second_half = vals[..., half_dim:].astype(jnp.float32)
    rotated = jnp.concatenate([first_half * cos_wide - second_half * sin_wide, second_half * cos_wide + first_half * sin_wide], axis=-1)
    return rotated.astype(jnp.bfloat16)


def attend(q_proj, k_proj, v_proj, allowed, cos_tab, sin_tab):
    n_blk = q_proj.shape[0]
    n_tok = q_proj.shape[1]
    kv_heads = k_proj.shape[2] // HEAD
    group_size = q_proj.shape[2] // k_proj.shape[2]
    q_rot = apply_rope(q_proj.reshape(n_blk, n_tok, kv_heads, group_size, HEAD), cos_tab, sin_tab)
    k_rot = apply_rope(k_proj.reshape(n_blk, n_tok, kv_heads, HEAD), cos_tab, sin_tab)
    v_heads = v_proj.reshape(n_blk, n_tok, kv_heads, HEAD)
    scores = jnp.einsum("btkgd,bskd->bkgts", q_rot, k_rot, preferred_element_type=jnp.float32) * HEAD ** -0.5
    scores = jnp.where(allowed, scores, -1e30)
    probs = jax.nn.softmax(scores, axis=-1).astype(jnp.bfloat16)
    mixed = jnp.einsum("bkgts,bskd->btkgd", probs, v_heads, preferred_element_type=jnp.float32)
    return mixed.astype(jnp.bfloat16).reshape(n_blk, n_tok, q_proj.shape[2])


def decoder_layer(hidden, allowed, cos_tab, sin_tab, w_q, w_k, w_v, w_o, w_gate, w_up, w_down, g_attn, g_mlp):
    normed = rms_norm(hidden, g_attn)
    q_proj = jnp.dot(normed, w_q, preferred_element_type=jnp.float32).astype(jnp.bfloat16)
    k_proj = jnp.dot(normed, w_k, preferred_element_type=jnp.float32).astype(jnp.bfloat16)
    v_proj = jnp.dot(normed, w_v, preferred_element_type=jnp.float32).astype(jnp.bfloat16)
    mixed = attend(q_proj, k_proj, v_proj, allowed, cos_tab, sin_tab)
    hidden = hidden + jnp.dot(mixed, w_o, preferred_element_type=jnp.float32)
    normed = rms_norm(hidden, g_mlp)
    gate_proj = jnp.dot(normed, w_gate, preferred_element_type=jnp.float32)
    up_proj = jnp.dot(normed, w_up, preferred_element_type=jnp.float32)
    act_val = (jax.nn.silu(gate_proj) * up_proj).astype(jnp.bfloat16)
    return hidden + jnp.dot(act_val, w_down, preferred_element_type=jnp.float32)


def gather_rows(w_shard):
    return lax.all_gather(w_shard, "fsdp", axis=0, tiled=True)


def solution(mesh):
    tok_spec = P(("rep", "fsdp"), None)
    seg_spec = P(("rep", "fsdp"))
    mat_spec = P(None, "fsdp", None)
    gain_spec = P(None, None)

    def per_device(tokens, seg_ids, w_q, w_k, w_v, w_o, w_gate, w_up, w_down, g_attn, g_mlp):
        n_tok, width = tokens.shape
        seg_blk = seg_ids.reshape(1, n_tok)
        cos_tab, sin_tab = rope_tables(seg_blk)
        allowed = attention_mask(seg_blk)
        hidden = tokens.astype(jnp.float32).reshape(1, n_tok, width)
        for layer in range(w_q.shape[0]):
            full_q = gather_rows(w_q[layer])
            full_k = gather_rows(w_k[layer])
            full_v = gather_rows(w_v[layer])
            full_o = gather_rows(w_o[layer])
            full_gate = gather_rows(w_gate[layer])
            full_up = gather_rows(w_up[layer])
            full_down = gather_rows(w_down[layer])
            hidden = decoder_layer(hidden, allowed, cos_tab, sin_tab, full_q, full_k, full_v, full_o, full_gate, full_up, full_down, g_attn[layer], g_mlp[layer])
        return hidden.reshape(n_tok, width)

    return jax.shard_map(per_device, mesh=mesh, in_specs=(tok_spec, seg_spec, mat_spec, mat_spec, mat_spec, mat_spec, mat_spec, mat_spec, mat_spec, gain_spec, gain_spec), out_specs=tok_spec, check_vma=False)
```

profile of v0, /device:TPU:0, one launch (start us, length us, event | category | flops | bytes accessed | tf_op | source)
XLA Modules:
  0.0 991.9 jit_solution(14168649866204848655)
XLA Ops:
  37.1 16.1 %all-gather.1 = bf16[1,1536,256]{2,1,0:T(8,128)(2,1)S(1)} all-gather(bf16[1,192,256]{2,1,0:T(8,128)(2,1)S(1)} %get-tuple-element.36), channel_id=3, replica_groups=mesh['rep'=1,'fsdp'=8] {'fsdp'}, dimensions={1}, use_global_device_ids=true | all-gather | bytes 884736 | tf_op jit(solution)/shard_map/all_gather | solution.py:75
  58.5 18.0 %all-gather = bf16[1,1536,256]{2,1,0:T(8,128)(2,1)S(1)} all-gather(bf16[1,192,256]{2,1,0:T(8,128)(2,1)S(1)} %get-tuple-element.38), channel_id=2, replica_groups=mesh['rep'=1,'fsdp'=8] {'fsdp'}, dimensions={1}, use_global_device_ids=true | all-gather | bytes 884736 | tf_op jit(solution)/shard_map/all_gather | solution.py:75
  81.0 13.3 %all-gather.8 = bf16[1,1536,256]{2,1,0:T(8,128)(2,1)} all-gather(bf16[1,192,256]{2,1,0:T(8,128)(2,1)S(1)} %get-tuple-element.35), channel_id=10, replica_groups=mesh['rep'=1,'fsdp'=8] {'fsdp'}, dimensions={1}, use_global_device_ids=true | all-gather | bytes 884736 | tf_op jit(solution)/shard_map/all_gather | solution.py:75
  94.3 18.6 %all-gather.7 = bf16[1,1536,256]{2,1,0:T(8,128)(2,1)} all-gather(bf16[1,192,256]{2,1,0:T(8,128)(2,1)S(1)} %get-tuple-element.37), channel_id=9, replica_groups=mesh['rep'=1,'fsdp'=8] {'fsdp'}, dimensions={1}, use_global_device_ids=true | all-gather | bytes 884736 | tf_op jit(solution)/shard_map/all_gather | solution.py:75
  115.2 9.6 fusion.63
  146.9 23.3 %fusion.2 = (f32[2,6,1024]{2,1,0:T(8,128)S(1)}, f32[2,1024,1024,6]{2,1,3,0:T(8,128)}) fusion(pred[1024,1024]{0,1:T(8,128)(4,1)S(1)} %fusion.60, bf16[1024,2,6,64]{3,0,2,1:T(8,128)(2,1)} %get-tuple-element.12, bf16[1024,2,6,64]{3,0,2,1:T(8,128)(2,1)S(1)} %get-tuple-element.11, bf16[1024,2,64]{2,0,1:T(8,128)(2,1)S(1)} %get-tuple-element.26, ...), kind=kOutput, calls=%fused_computation.8 | convolution fusion | flops 3266301952 | bytes 55099392 | tf_op jit(solution)/shard_map/btkgd,bskd->bkgts/dot_general | solution.py:53
  170.1 21.3 %fusion = f32[2,6,1024]{2,1,0:T(8,128)S(1)} fusion(f32[2,1024,1024,6]{2,1,3,0:T(8,128)} %get-tuple-element.42, f32[2,6,1024]{2,1,0:T(8,128)S(1)} %get-tuple-element.41, pred[1024,1024]{0,1:T(8,128)(4,1)S(1)} %fusion.60), kind=kLoop, calls=%fused_computation.6 | loop fusion | flops 50319360 | bytes 51478528 | tf_op jit(solution)/shard_map/reduce_sum | solution.py:55
  191.4 23.3 %fusion.87 = bf16[2,128,6,1024]{3,1,2,0:T(8,128)(2,1)} fusion(bf16[1024,2,128,1]{0,2,3,1:T(8,128)(2,1)S(1)} %bitcast.207, f32[2,6,1024]{2,1,0:T(8,128)S(1)} %fusion, f32[2,6,1024]{2,1,0:T(8,128)S(1)} %get-tuple-element.41, f32[2,1024,1024,6]{2,1,3,0:T(8,128)} %get-tuple-element.42, pred[1024,1024]{0,1:T(8,128)(4,1)S(1)} %fusion.60), kind=kOutput, calls=%fused_computation.87 | convolution fusion | flops 3285712896 | bytes 55148544 | tf_op jit(solution)/shard_map/bkgts,bskd->btkgd/dot_general | solution.py:56
  214.7 10.6 %multiply_reduce_fusion.2 = (f32[1024]{0:T(1024)S(1)}, f32[1024,1536]{1,0:T(8,128)}) fusion(bf16[1024,1536]{0,1:T(8,128)(2,1)} %bitcast.206, bf16[1,1536,1536]{2,1,0:T(8,128)(2,1)} %all-gather.27.cloned.1.call-done, bf16[1024,1536]{1,0:T(8,128)(2,1)} %param.11), kind=kOutput, calls=%fused_computation.55 | convolution fusion | flops 4838128640 | bytes 17305600 | tf_op jit(solution)/shard_map/dot_general | solution.py:66
  225.3 37.0 %fusion.12 = f32[1024,8960]{1,0:T(8,128)} fusion(bf16[1,1536,8960]{2,1,0:T(8,128)(2,1)} %all-gather.31.cloned.1.call-done, f32[1024,1536]{1,0:T(8,128)} %get-tuple-element.44, f32[1536]{0:T(1024)S(1)} %get-tuple-element.6, f32[1024]{0:T(1024)S(1)} %add_rsqrt_fusion.2), kind=kOutput, calls=%fused_computation.20 | convolution fusion | flops 28190441472 | bytes 70526976 | tf_op jit(solution)/shard_map/dot_general | solution.py:69
  262.3 88.9 %all-gather.29.cloned.1.call-done = bf16[1,1536,8960]{2,1,0:T(8,128)(2,1)} async-done(((bf16[1,192,8960]{2,1,0:T(8,128)(2,1)}), bf16[1,1536,8960]{2,1,0:T(8,128)(2,1)}) %all-gather.29.cloned.1.call-update) | async-done | bytes 27525136 | tf_op jit(solution)/shard_map/all_gather | solution.py:75
  351.2 41.3 %multiply_convert_fusion.8.clone.4 = bf16[1024,8960]{1,0:T(8,128)(2,1)} fusion(f32[1024,8960]{1,0:T(8,128)} %fusion.12, bf16[1,1536,8960]{2,1,0:T(8,128)(2,1)} %all-gather.29.cloned.1.call-done, f32[1024,1536]{1,0:T(8,128)} %get-tuple-element.44, f32[1536]{0:T(1024)S(1)} %get-tuple-element.6, f32[1024]{0:T(1024)S(1)} %add_rsqrt_fusion.2), kind=kOutput, calls=%fused_computation.11.clone.clone.clone.clone.clone.clone.1 | convolution fusion | flops 28245491712 | bytes 88877056 | tf_op jit(solution)/shard_map/dot_general | solution.py:68
  392.5 90.1 %all-gather.33.cloned.1.call-done = bf16[1,8960,1536]{2,1,0:T(8,128)(2,1)} async-done(((bf16[1,1120,1536]{2,1,0:T(8,128)(2,1)}), bf16[1,8960,1536]{2,1,0:T(8,128)(2,1)}) %all-gather.33.cloned.1.call-update) | async-done | bytes 27525136 | tf_op jit(solution)/shard_map/all_gather | solution.py:75
  482.5 36.2 %multiply_reduce_fusion.1 = (f32[1024]{0:T(1024)S(1)}, f32[1024,1536]{1,0:T(8,128)S(1)}) fusion(f32[1024,1536]{1,0:T(8,128)} %get-tuple-element.44, bf16[1,8960,1536]{2,1,0:T(8,128)(2,1)} %all-gather.33.cloned.1.call-done, bf16[1024,8960]{1,0:T(8,128)(2,1)} %multiply_convert_fusion.8.clone.4), kind=kOutput, calls=%fused_computation.53 | convolution fusion | flops 28190441472 | bytes 58462208 | tf_op jit(solution)/shard_map/dot_general | solution.py:71
  555.2 23.3 %fusion.3 = (f32[2,6,1024]{2,1,0:T(8,128)S(1)}, f32[2,1024,1024,6]{2,1,3,0:T(8,128)}) fusion(pred[1024,1024]{0,1:T(8,128)(4,1)S(1)} %copy-done.1, bf16[1024,2,6,64]{3,0,2,1:T(8,128)(2,1)} %get-tuple-element.10, bf16[1024,2,6,64]{3,0,2,1:T(8,128)(2,1)S(1)} %get-tuple-element.9, bf16[1024,2,64]{2,0,1:T(8,128)(2,1)S(1)} %get-tuple-element.24, ...), kind=kOutput, calls=%fused_computation.9 | convolution fusion | flops 3266301952 | bytes 55099392 | tf_op jit(solution)/shard_map/btkgd,bskd->bkgts/dot_general | solution.py:53
  578.5 21.2 %fusion.1 = f32[2,6,1024]{2,1,0:T(8,128)S(1)} fusion(f32[2,1024,1024,6]{2,1,3,0:T(8,128)} %get-tuple-element.48, f32[2,6,1024]{2,1,0:T(8,128)S(1)} %get-tuple-element.47, pred[1024,1024]{0,1:T(8,128)(4,1)S(1)} %copy-done.1), kind=kLoop, calls=%fused_computation.7 | loop fusion | flops 50319360 | bytes 51478528 | tf_op jit(solution)/shard_map/reduce_sum | solution.py:55
  599.7 23.4 %fusion.90 = bf16[2,128,6,1024]{3,1,2,0:T(8,128)(2,1)} fusion(bf16[1024,2,128,1]{0,2,3,1:T(8,128)(2,1)S(1)} %bitcast.208, f32[2,6,1024]{2,1,0:T(8,128)S(1)} %fusion.1, f32[2,6,1024]{2,1,0:T(8,128)S(1)} %get-tuple-element.47, f32[2,1024,1024,6]{2,1,3,0:T(8,128)} %get-tuple-element.48, pred[1024,1024]{0,1:T(8,128)(4,1)S(1)} %copy-done.1), kind=kOutput, calls=%fused_computation.88 | convolution fusion | flops 3285712896 | bytes 55148544 | tf_op jit(solution)/shard_map/bkgts,bskd->btkgd/dot_general | solution.py:56
  623.1 10.9 %multiply_reduce_fusion = (f32[1024]{0:T(1024)S(1)}, f32[1024,1536]{1,0:T(8,128)}) fusion(f32[1024,1536]{1,0:T(8,128)} %copy-done.2, bf16[1024,1536]{0,1:T(8,128)(2,1)} %bitcast.200, bf16[1,1536,1536]{2,1,0:T(8,128)(2,1)} %all-gather.37.cloned.1.call-done), kind=kOutput, calls=%fused_computation.51 | convolution fusion | flops 4836555776 | bytes 20451328 | tf_op jit(solution)/shard_map/dot_general | solution.py:66
  634.0 49.4 %all-gather.41.cloned.1.call-done = bf16[1,1536,8960]{2,1,0:T(8,128)(2,1)} async-done(((bf16[1,192,8960]{2,1,0:T(8,128)(2,1)}), bf16[1,1536,8960]{2,1,0:T(8,128)(2,1)}) %all-gather.41.cloned.1.call-update) | async-done | bytes 27525136 | tf_op jit(solution)/shard_map/all_gather | solution.py:75
  683.5 37.0 %fusion.6 = f32[1024,8960]{1,0:T(8,128)} fusion(bf16[1,1536,8960]{2,1,0:T(8,128)(2,1)} %all-gather.41.cloned.1.call-done, f32[1024,1536]{1,0:T(8,128)} %get-tuple-element.50, f32[1536]{0:T(1024)S(1)} %copy-done.23, f32[1024]{0:T(1024)S(1)} %add_rsqrt_fusion), kind=kOutput, calls=%fused_computation.14 | convolution fusion | flops 28190441472 | bytes 70526976 | tf_op jit(solution)/shard_map/dot_general | solution.py:69
  720.4 94.5 %all-gather.39.cloned.1.call-done = bf16[1,1536,8960]{2,1,0:T(8,128)(2,1)} async-done(((bf16[1,192,8960]{2,1,0:T(8,128)(2,1)}), bf16[1,1536,8960]{2,1,0:T(8,128)(2,1)}) %all-gather.39.cloned.1.call-update) | async-done | bytes 27525136 | tf_op jit(solution)/shard_map/all_gather | solution.py:75
  815.0 40.8 %multiply_convert_fusion.27 = bf16[1024,8960]{1,0:T(8,128)(2,1)} fusion(f32[1024,8960]{1,0:T(8,128)} %fusion.6, bf16[1,1536,8960]{2,1,0:T(8,128)(2,1)} %all-gather.39.cloned.1.call-done, f32[1024,1536]{1,0:T(8,128)} %get-tuple-element.50, f32[1536]{0:T(1024)S(1)} %copy-done.23, f32[1024]{0:T(1024)S(1)} %add_rsqrt_fusion), kind=kOutput, calls=%fused_computation.10.clone.clone.clone.clone.1 | convolution fusion | flops 28245491712 | bytes 88877056 | tf_op jit(solution)/shard_map/dot_general | solution.py:68
  855.8 90.5 %all-gather.43.cloned.1.call-done = bf16[1,8960,1536]{2,1,0:T(8,128)(2,1)} async-done(((bf16[1,1120,1536]{2,1,0:T(8,128)(2,1)}), bf16[1,8960,1536]{2,1,0:T(8,128)(2,1)}) %all-gather.43.cloned.1.call-update) | async-done | bytes 27525136 | tf_op jit(solution)/shard_map/all_gather | solution.py:75
  946.3 38.4 %fusion.52 = f32[1024,1536]{1,0:T(8,128)} fusion(f32[1024,1536]{1,0:T(8,128)} %get-tuple-element.50, bf16[1,8960,1536]{2,1,0:T(8,128)(2,1)} %all-gather.43.cloned.1.call-done, bf16[1024,8960]{1,0:T(8,128)(2,1)} %multiply_convert_fusion.27), kind=kOutput, calls=%fused_computation.65 | convolution fusion | flops 28187295744 | bytes 58458112 | tf_op jit(solution)/shard_map/dot_general | solution.py:71
  (126 shorter events, 100.8 us)
Async XLA Ops:
  6.5 108.6 %all-gather.25.cloned.1.call-start = ((), (), s32[]{:S(2)}) async-start(), calls=%async_computation | async-start | bytes 5308416 | tf_op jit(solution)/shard_map/all_gather | solution.py:75
  8.9 205.8 %all-gather.27.cloned.1.call-start = ((), (), s32[]{:S(2)}) async-start(), calls=%async_computation.1 | async-start | bytes 5308416 | tf_op jit(solution)/shard_map/all_gather | solution.py:75
  11.3 214.0 %all-gather.31.cloned.1.call-start = ((), (), s32[]{:S(2)}) async-start(), calls=%async_computation.3 | async-start | bytes 30965760 | tf_op jit(solution)/shard_map/all_gather | solution.py:75
  17.7 333.5 %all-gather.29.cloned.1.call-start = ((), (), s32[]{:S(2)}) async-start(), calls=%async_computation.2 | async-start | bytes 30965760 | tf_op jit(solution)/shard_map/all_gather | solution.py:75
  24.1 458.5 %all-gather.33.cloned.1.call-start = ((), (), s32[]{:S(2)}) async-start(), calls=%async_computation.4 | async-start | bytes 30965760 | tf_op jit(solution)/shard_map/all_gather | solution.py:75
  30.8 494.7 %all-gather.35.cloned.1.call-start = ((), (), s32[]{:S(2)}) async-start(), calls=%async_computation.5 | async-start | bytes 5308416 | tf_op jit(solution)/shard_map/all_gather | solution.py:75
  31.4 591.7 %all-gather.37.cloned.1.call-start = ((), (), s32[]{:S(2)}) async-start(), calls=%async_computation.6 | async-start | bytes 5308416 | tf_op jit(solution)/shard_map/all_gather | solution.py:75
  32.1 651.3 %all-gather.41.cloned.1.call-start = ((), (), s32[]{:S(2)}) async-start(), calls=%async_computation.8 | async-start | bytes 30965760 | tf_op jit(solution)/shard_map/all_gather | solution.py:75
  32.9 782.1 %all-gather.39.cloned.1.call-start = ((), (), s32[]{:S(2)}) async-start(), calls=%async_computation.7 | async-start | bytes 30965760 | tf_op jit(solution)/shard_map/all_gather | solution.py:75
  33.6 912.7 %all-gather.43.cloned.1.call-start = ((), (), s32[]{:S(2)}) async-start(), calls=%async_computation.9 | async-start | bytes 30965760 | tf_op jit(solution)/shard_map/all_gather | solution.py:75
  35.6 22.9 %copy-start.18 = (bf16[2,192,256]{2,1,0:T(8,128)(2,1)S(1)}, bf16[2,192,256]{2,1,0:T(8,128)(2,1)}, u32[]{:S(2)}) copy-start(bf16[2,192,256]{2,1,0:T(8,128)(2,1)} %param.15) | copy-start | bytes 589828
  36.2 155.2 %copy-start = (pred[1024,1024]{0,1:T(8,128)(4,1)}, pred[1024,1024]{0,1:T(8,128)(4,1)S(1)}, u32[]{:S(2)}) copy-start(pred[1024,1024]{0,1:T(8,128)(4,1)S(1)} %fusion.60) | copy-start | bytes 3145732
  56.4 24.0 %copy-start.22 = (bf16[2,1536]{1,0:T(2,128)(2,1)S(1)}, bf16[2,1536]{1,0:T(2,128)(2,1)}, u32[]{:S(2)}) copy-start(bf16[2,1536]{1,0:T(2,128)(2,1)} %param.21) | copy-start | bytes 18436
  58.5 56.3 %copy-start.11 = (bf16[1,1024,2,64]{3,1,2,0:T(8,128)(2,1)S(1)}, bf16[1,1024,2,64]{3,1,2,0:T(8,128)(2,1)}, u32[]{:S(2)}) copy-start(bf16[1,1024,2,64]{3,1,2,0:T(8,128)(2,1)} %copy.36) | copy-start | bytes 786436
  58.5 56.3 %copy-start.12 = (bf16[1,1024,2,64]{3,1,2,0:T(8,128)(2,1)S(1)}, bf16[1,1024,2,64]{3,1,2,0:T(8,128)(2,1)}, u32[]{:S(2)}) copy-start(bf16[1,1024,2,64]{3,1,2,0:T(8,128)(2,1)} %copy.37) | copy-start | bytes 786436
  114.8 27.0 %copy-start.3 = (f32[1024,64]{1,0:T(8,128)}, f32[1024,64]{1,0:T(8,128)S(1)}, u32[]{:S(2)}) copy-start(f32[1024,64]{1,0:T(8,128)S(1)} %get-tuple-element.39) | copy-start | bytes 786436
  114.8 27.0 %copy-start.5 = (f32[1024,64]{1,0:T(8,128)}, f32[1024,64]{1,0:T(8,128)S(1)}, u32[]{:S(2)}) copy-start(f32[1024,64]{1,0:T(8,128)S(1)} %get-tuple-element.40) | copy-start | bytes 786436
  170.1 21.3 %copy-start.24 = (bf16[1024,256]{0,1:T(8,128)(2,1)S(1)}, bf16[1024,256]{0,1:T(8,128)(2,1)}, u32[]{:S(2)}) copy-start(bf16[1024,256]{0,1:T(8,128)(2,1)} %convolution_convert_fusion.3) | copy-start | bytes 1572868
  392.5 126.4 %copy-start.20 = (f32[1536]{0:T(1024)S(1)}, f32[1536]{0:T(1024)}, u32[]{:S(2)}) copy-start(f32[1536]{0:T(1024)} %get-tuple-element.7) | copy-start | bytes 18436
  539.6 8.5 copy-start.6
  539.6 8.5 copy-start.13
  539.6 8.5 copy-start.14
  539.6 8.9 copy-start.15
  623.1 60.3 %copy-start.23 = (f32[1536]{0:T(1024)S(1)}, f32[1536]{0:T(1024)}, u32[]{:S(2)}) copy-start(f32[1536]{0:T(1024)} %get-tuple-element.5) | copy-start | bytes 18436
  (11 other events, 43.6 us)
Sparse Core Ops, SparseCore 0:
  9.1 35.7 all-gather.24
  46.8 36.6 all-gather.26
  85.3 134.5 all-gather.30
  221.5 129.6 all-gather.28
  352.9 129.6 all-gather.32
  484.2 32.9 all-gather.34
  519.0 32.9 all-gather.36
  553.8 129.6 all-gather.40
  685.3 129.6 all-gather.38
  816.6 129.6 all-gather.42
where the time goes:
time: 1000 us; the launch traced here: 992 us
  waiting for transfers between devices  417 us (42%)
  matrix products  375 us (38%)
  blocking collectives  65.9 us (7%)
  local copies, waits for them, and re-layouts  62.5 us (6%)
  other arithmetic  57.3 us (6%)
  between operations  14.4 us (1%)
    all_gather x10, waiting for transfers between devices, gather_rows(): return lax.all_gather(w_shard, 'fsdp', axis=0, tiled=True)  413 us
    dot_general x2, matrix products, decoder_layer(): gate_proj = jnp.dot(normed, w_gate, preferred_element_type=jnp.float32)  82.1 us
    dot_general x2, matrix products, decoder_layer(): return hidden + jnp.dot(act_val, w_down, preferred_element_type=jnp.float32)  74.6 us
    dot_general x2, matrix products, decoder_layer(): up_proj = jnp.dot(normed, w_up, preferred_element_type=jnp.float32)  73.9 us
    all_gather x4, blocking collectives, gather_rows(): return lax.all_gather(w_shard, 'fsdp', axis=0, tiled=True)  65.9 us
    dot_general x2, matrix products, attend(): jnp.einsum('bkgts,bskd->btkgd', probs, v_heads, preferred_element_type=jn...  46.7 us
    dot_general x2, matrix products, attend(): jnp.einsum('btkgd,bskd->bkgts', q_rot, k_rot, preferred_element_type=jnp....  46.5 us
    reduce_sum x2, other arithmetic, attend(): probs = jax.nn.softmax(scores, axis=-1).astype(jnp.bfloat16)  42.5 us
  transfers between devices with their start and end apart: 10, of which 5 were waited for; matrix products, arithmetic and copies ran while one was open for 46% of the time, Pallas kernels for 0%

commit v1 on v0

v1 whole, which is shorter than its diff:
```python
import functools

import jax
import jax.numpy as jnp
from jax import lax
from jax.experimental import pallas as pl
from jax.experimental.pallas import tpu as pltpu
from jax.sharding import PartitionSpec as P

HEAD = 128
HEADS = 12
KV_HEADS = 2
EPS = 1e-5
ROPE_BASE = 10000.0
MESH = pl.DeviceIdType.MESH

N_DEV = 8
TOK = 1024
D = 1536
KV = KV_HEADS * HEAD
FF = 8960
ROWS = D // N_DEV
FROWS = FF // N_DEV
TF = 640
N_GU = FF // TF
DR = 160
N_DN = FROWS // DR
PER = 2 + N_DN + N_GU
GU0 = 2 + N_DN
LAYERS = 2
TOTAL = PER * LAYERS
RING = 8
MB = 256
SCALE = HEAD ** -0.5


def kernel(tok, seg_c, seg_r, freq, g_attn, g_mlp, w_q, w_k, w_v, w_o, w_g, w_u, w_d,
           out, f_q, f_k, f_v, f_o, f_g, f_u, f_d,
           x, h, q, k, v, o, cos_t, sin_t, mask, vq, vk, vv, vo, vg, vu, vd,
           b_q, b_k, b_v, b_o, b_g, b_u, b_d,
           send, recv, loc, ld):
    me = lax.axis_index("fsdp")
    core = lax.rem(me, 2)
    xc = lax.rem(me // 2, 2)
    yc = me // 4
    xn = me + 2 - 4 * xc
    yn = me + 4 - 8 * yc
    cn = me + 1 - 2 * core
    dg = xn + 4 - 8 * yc

    barrier = pltpu.get_barrier_semaphore()
    for nb in (xn, yn, cn):
        pl.semaphore_signal(barrier, inc=1, device_id={"fsdp": nb}, device_id_type=MESH)
    pl.semaphore_wait(barrier, 3)

    def pieces(rd):
        kind, l, j = rd
        if kind == "qkv":
            return [(w_q, f_q, ROWS, ROWS, 0, 0, D, b_q), (w_k, f_k, ROWS, ROWS, 0, 0, KV, b_k), (w_v, f_v, ROWS, ROWS, 0, 0, KV, b_v)]
        if kind == "o":
            return [(w_o, f_o, ROWS, ROWS, 0, 0, D, b_o)]
        par = lax.rem(j, 4)
        if kind == "dn":
            return [(w_d, f_d, FROWS, DR, j * DR, 0, D, b_d.at[par])]
        return [(w_g, f_g, ROWS, ROWS, 0, j * TF, TF, b_g.at[par]), (w_u, f_u, ROWS, ROWS, 0, j * TF, TF, b_u.at[par])]

    def al(i, n):
        return i if isinstance(i, int) else pl.multiple_of(i, n)

    def own_view(p, l):
        src, _, _, nr, r0, c0, nc, _ = p
        return src.at[l, pl.ds(al(r0, 16), nr), pl.ds(al(c0, 128), nc)]

    def gview(p, l, dev, half=None):
        _, dst, span, nr, r0, c0, nc, _ = p
        off, n = {None: (0, nr), "A": (0, nr // 2), "B": (nr // 2, nr // 2)}[half]
        return dst.at[l, pl.ds(al(dev * span + r0 + off, 16), n), pl.ds(al(c0, 128), nc)]

    def tx(p, l, slot, m, t):
        if t == 0:
            s, d, dev = own_view(p, l), gview(p, l, me), xn
        elif t == 1:
            s, d, dev = own_view(p, l), gview(p, l, me), yn
        elif t == 2:
            s, d, dev = own_view(p, l), gview(p, l, me), cn
        else:
            owner, half, dev = {3: (yn, "A", xn), 4: (xn, "B", yn), 5: (xn, None, cn), 6: (yn, None, cn), 7: (dg, "A", cn), 8: (dg, "B", cn)}[t]
            s = gview(p, l, owner, half)
            d = s
        return pltpu.make_async_remote_copy(src_ref=s, dst_ref=d, send_sem=send.at[slot, m, t], recv_sem=recv.at[slot, m, t],
                                            device_id={"fsdp": dev}, device_id_type=MESH)

    def bounce_in(p, l, slot, m):
        return pltpu.make_async_copy(own_view(p, l), p[7], loc.at[slot, m, 0])

    def bounce_out(p, l, slot, m):
        return pltpu.make_async_copy(p[7], gview(p, l, me), loc.at[slot, m, 1])

    def step_e(rd, slot):
        for m, p in enumerate(pieces(rd)):
            for t in (0, 1, 2):
                tx(p, rd[1], slot, m, t).start()
            bounce_in(p, rd[1], slot, m).start()

    def step_a(rd, slot):
        for m, p in enumerate(pieces(rd)):
            tx(p, rd[1], slot, m, 0).wait_recv()
            tx(p, rd[1], slot, m, 4).start()
            tx(p, rd[1], slot, m, 5).start()
            tx(p, rd[1], slot, m, 1).wait_recv()
            tx(p, rd[1], slot, m, 3).start()
            tx(p, rd[1], slot, m, 6).start()
            bounce_in(p, rd[1], slot, m).wait()
            bounce_out(p, rd[1], slot, m).start()

    def step_b(rd, slot):
        for m, p in enumerate(pieces(rd)):
            tx(p, rd[1], slot, m, 3).wait_recv()
            tx(p, rd[1], slot, m, 7).start()
            tx(p, rd[1], slot, m, 4).wait_recv()
            tx(p, rd[1], slot, m, 8).start()

    def step_c(rd, slot):
        for m, p in enumerate(pieces(rd)):
            for t in (2, 5, 6, 7, 8):
                tx(p, rd[1], slot, m, t).wait_recv()
            for t in range(9):
                tx(p, rd[1], slot, m, t).wait_send()
            bounce_out(p, rd[1], slot, m).wait()

    STEPS = ((step_c, -3), (step_b, -2), (step_a, -1), (step_e, 1))

    def round_of(r):
        l, i = divmod(r, PER)
        if i == 0:
            return ("qkv", l, 0)
        if i == 1:
            return ("o", l, 0)
        if i < GU0:
            return ("dn", l, i - 2)
        return ("gu", l, i - GU0)

    def service(r):
        for fn, off in STEPS:
            if 0 <= r + off < TOTAL:
                fn(round_of(r + off), (r + off) % RING)

    def service_loop(l, t):
        for fn, off in STEPS:
            lag = 3 + off
            base = PER * l + GU0

            def dyn(fn=fn, lag=lag, base=base):
                fn(("gu", l, t + lag), lax.rem(base + lag + t, RING))

            if lag == 0:
                dyn()
                continue
            pl.when(t + lag < N_GU)(dyn)
            for kk in range(lag):
                r = PER * (l + 1) + kk
                if r < TOTAL:
                    def stat(fn=fn, r=r):
                        fn(round_of(r), r % RING)
                    pl.when(t == N_GU + kk - lag)(stat)

    step_e(round_of(0), 0)
    tok_in = pltpu.make_async_copy(tok, o, ld.at[0])
    tok_in.start()
    service(0)

    def tables(i, c):
        rows = pl.ds(pl.multiple_of(i * MB, MB), MB)
        same = seg_c[rows, :] == seg_r[...]
        rr = lax.broadcasted_iota(jnp.int32, (MB, TOK), 0) + i * MB
        cc = lax.broadcasted_iota(jnp.int32, (MB, TOK), 1)
        ok = jnp.where(same & (cc <= rr), 1.0, 0.0)
        mask[rows, :] = ok
        pos = jnp.sum(ok, axis=1, keepdims=True) - 1.0
        ang = pos * freq[...]
        lane = lax.broadcasted_iota(jnp.int32, (MB, HEAD), 1)
        cos_t[rows, :] = jnp.cos(ang)
        sn = jnp.sin(ang)
        sin_t[rows, :] = jnp.where(lane < HEAD // 2, -sn, sn)
        return c

    lax.fori_loop(0, TOK // MB, tables, 0)
    tok_in.wait()

    def widen(i, c):
        rows = pl.ds(pl.multiple_of(i * MB, MB), MB)
        x[rows, :] = o[rows, :].astype(jnp.float32)
        return c

    lax.fori_loop(0, TOK // MB, widen, 0)

    def norm_rows(gain_ref, l):
        def body(i, c):
            rows = pl.ds(pl.multiple_of(i * MB, MB), MB)
            xv = x[rows, :]
            inv = lax.rsqrt(jnp.mean(xv * xv, axis=-1, keepdims=True) + EPS)
            h[rows, :] = (xv * inv * gain_ref[l:l + 1, :].astype(jnp.float32)).astype(jnp.bfloat16)
            return c
        lax.fori_loop(0, TOK // MB, body, 0)

    def rope(val, rows):
        f = val.astype(jnp.bfloat16).astype(jnp.float32)
        return (f * cos_t[rows, :] + pltpu.roll(f, HEAD // 2, 1) * sin_t[rows, :]).astype(jnp.bfloat16)

    def qkv_rows(i, c):
        rows = pl.ds(pl.multiple_of(i * MB, MB), MB)
        hv = h[rows, :]
        for g in range(HEADS // 4):
            val = jnp.dot(hv, vq[:, g * 512:(g + 1) * 512], preferred_element_type=jnp.float32)
            for e in range(4):
                q[rows, g * 512 + e * HEAD:g * 512 + (e + 1) * HEAD] = rope(val[:, e * HEAD:(e + 1) * HEAD], rows)
        val = jnp.dot(hv, vk[...], preferred_element_type=jnp.float32)
        for e in range(KV_HEADS):
            k[rows, e * HEAD:(e + 1) * HEAD] = rope(val[:, e * HEAD:(e + 1) * HEAD], rows)
        v[rows, :] = jnp.dot(hv, vv[...], preferred_element_type=jnp.float32).astype(jnp.bfloat16)
        return c

    def head_body(hd, c):
        qc = pl.ds(pl.multiple_of(hd * HEAD, HEAD), HEAD)
        kc = pl.ds(pl.multiple_of((hd // (HEADS // KV_HEADS)) * HEAD, HEAD), HEAD)
        for i in range(TOK // MB):
            n = (i + 1) * MB
            s = lax.dot_general(q[i * MB:n, qc], k[0:n, kc], (((1,), (1,)), ((), ())), preferred_element_type=jnp.float32) * SCALE
            s = jnp.where(mask[i * MB:n, 0:n] > 0.5, s, -1e30)
            e = jnp.exp(s - jnp.max(s, axis=1, keepdims=True))
            p = (e / jnp.sum(e, axis=1, keepdims=True)).astype(jnp.bfloat16)
            o[i * MB:n, qc] = jnp.dot(p, v[0:n, kc], preferred_element_type=jnp.float32).astype(jnp.bfloat16)
        return c

    def proj_rows(i, c):
        rows = pl.ds(pl.multiple_of(i * MB, MB), MB)
        x[rows, :] += jnp.dot(o[rows, :], vo[...], preferred_element_type=jnp.float32)
        return c

    def mlp_rows(i, c):
        rows = pl.ds(pl.multiple_of(i * MB, MB), MB)
        hv = h[rows, :]
        gt = jnp.dot(hv, vg[...], preferred_element_type=jnp.float32)
        up = jnp.dot(hv, vu[...], preferred_element_type=jnp.float32)
        a = (gt * jax.nn.sigmoid(gt) * up).astype(jnp.bfloat16)
        x[rows, :] += jnp.dot(a, vd[...], preferred_element_type=jnp.float32)
        return c

    for l in range(LAYERS):
        if l == 0:
            for r in range(1, 3):
                service(r)
        norm_rows(g_attn, l)
        base = PER * l
        service(base + 3)
        loads = [pltpu.make_async_copy(f_q.at[l], vq, ld.at[0]), pltpu.make_async_copy(f_k.at[l], vk, ld.at[1]), pltpu.make_async_copy(f_v.at[l], vv, ld.at[2])]
        for c in loads:
            c.start()
        for c in loads:
            c.wait()
        lax.fori_loop(0, TOK // MB, qkv_rows, 0)
        service(base + 4)
        load_o = pltpu.make_async_copy(f_o.at[l], vo, ld.at[0])
        load_o.start()
        per_group = HEADS // 6
        for g in range(6):
            lax.fori_loop(g * per_group, (g + 1) * per_group, head_body, 0)
            service(base + 5 + g)
        load_o.wait()
        lax.fori_loop(0, TOK // MB, proj_rows, 0)
        norm_rows(g_mlp, l)
        for r in range(base + 11, base + GU0 + 3):
            service(r)

        def tile(t, c):
            service_loop(l, t)
            cols = pl.ds(pl.multiple_of(t * TF, 128), TF)
            loads = [pltpu.make_async_copy(f_g.at[l, :, cols], vg, ld.at[0]), pltpu.make_async_copy(f_u.at[l, :, cols], vu, ld.at[1]), pltpu.make_async_copy(f_d.at[l, cols, :], vd, ld.at[2])]
            for cp in loads:
                cp.start()
            for cp in loads:
                cp.wait()
            lax.fori_loop(0, TOK // MB, mlp_rows, 0)
            return c

        lax.fori_loop(0, N_GU, tile, 0)
    done = pltpu.make_async_copy(x, out, ld.at[0])
    done.start()
    done.wait()


def solution(mesh):
    tok_spec = P(("rep", "fsdp"), None)
    seg_spec = P(("rep", "fsdp"))
    mat_spec = P(None, "fsdp", None)
    gain_spec = P(None, None)
    bf, f32 = jnp.bfloat16, jnp.float32

    def per_device(tokens, seg_ids, w_q, w_k, w_v, w_o, w_gate, w_up, w_down, g_attn, g_mlp):
        half = HEAD // 2
        inv = ROPE_BASE ** (-jnp.arange(half, dtype=f32) / half)
        freq = jnp.concatenate([inv, inv]).reshape(1, HEAD)
        any_s = pl.BlockSpec(memory_space=pl.ANY)
        vm = pl.BlockSpec(memory_space=pltpu.VMEM)
        full = [(LAYERS, D, D), (LAYERS, D, KV), (LAYERS, D, KV), (LAYERS, D, D), (LAYERS, D, FF), (LAYERS, D, FF), (LAYERS, FF, D)]
        res = pl.pallas_call(
            kernel,
            out_shape=[jax.ShapeDtypeStruct((TOK, D), f32)] + [jax.ShapeDtypeStruct(s, bf) for s in full],
            in_specs=[any_s, vm, vm, vm, vm, vm] + [any_s] * 7,
            out_specs=[any_s] * 8,
            scratch_shapes=[
                pltpu.VMEM((TOK, D), f32), pltpu.VMEM((TOK, D), bf), pltpu.VMEM((TOK, D), bf),
                pltpu.VMEM((TOK, KV), bf), pltpu.VMEM((TOK, KV), bf), pltpu.VMEM((TOK, D), bf),
                pltpu.VMEM((TOK, HEAD), f32), pltpu.VMEM((TOK, HEAD), f32), pltpu.VMEM((TOK, TOK), f32),
                pltpu.VMEM((D, D), bf), pltpu.VMEM((D, KV), bf), pltpu.VMEM((D, KV), bf), pltpu.VMEM((D, D), bf),
                pltpu.VMEM((D, TF), bf), pltpu.VMEM((D, TF), bf), pltpu.VMEM((TF, D), bf),
                pltpu.VMEM((ROWS, D), bf), pltpu.VMEM((ROWS, KV), bf), pltpu.VMEM((ROWS, KV), bf), pltpu.VMEM((ROWS, D), bf),
                pltpu.VMEM((4, ROWS, TF), bf), pltpu.VMEM((4, ROWS, TF), bf), pltpu.VMEM((4, DR, D), bf),
                pltpu.SemaphoreType.DMA((RING, 3, 9)), pltpu.SemaphoreType.DMA((RING, 3, 9)),
                pltpu.SemaphoreType.DMA((RING, 3, 2)), pltpu.SemaphoreType.DMA((4,)),
            ],
            compiler_params=pltpu.CompilerParams(collective_id=0, has_side_effects=True, vmem_limit_bytes=66 * 1000 * 1000),
        )(tokens, seg_ids.reshape(TOK, 1), seg_ids.reshape(1, TOK), freq, g_attn, g_mlp, w_q, w_k, w_v, w_o, w_gate, w_up, w_down)
        return res[0]

    return jax.shard_map(per_device, mesh=mesh, in_specs=(tok_spec, seg_spec, mat_spec, mat_spec, mat_spec, mat_spec, mat_spec, mat_spec, mat_spec, gain_spec, gain_spec), out_specs=tok_spec, check_vma=False)
```

time: 1000 us -> 801 us (0.80)
  Pallas kernels: 0 us -> 793 us
  waiting for transfers between devices: 417 us -> 0 us
  matrix products: 375 us -> 0 us
  blocking collectives: 65.9 us -> 0 us
  other arithmetic: 57.3 us -> 0.6 us
  local copies, waits for them, and re-layouts: 62.5 us -> 7.64 us
  between operations: 14.4 us -> 0.01 us
    pallas_call x0 -> x1, Pallas kernels: none -> 793 us  [per_device(): pl.pallas_call(kernel, out_shape=[jax.ShapeDtypeStruct((TOK, D), f32)] +...]
    all_gather x10 -> x0, waiting for transfers between devices: 413 us -> none  [gather_rows(): return lax.all_gather(w_shard, 'fsdp', axis=0, tiled=True)]
    dot_general x18 -> x0, matrix products: 375 us -> none  [the longest x2 82.1 us: decoder_layer(): gate_proj = jnp.dot(normed, w_gate, preferred_element_type=jnp.float32)]
    all_gather x4 -> x0, blocking collectives: 65.9 us -> none  [gather_rows(): return lax.all_gather(w_shard, 'fsdp', axis=0, tiled=True)]
    reduce_sum x3 -> x0, other arithmetic: 43.2 us -> none  [the longest x2 42.5 us: attend(): probs = jax.nn.softmax(scores, axis=-1).astype(jnp.bfloat16)]
    slice x13 -> x0, local copies, waits for them, and re-layouts: 31.3 us -> none  [the longest x4 7.14 us: apply_rope(): second_half = vals[..., half_dim:].astype(jnp.float32)]
    unnamed x58 -> x1, local copies, waits for them, and re-layouts: 23.2 us -> 5.93 us
  transfers between devices with their start and end apart: 10 -> 0, of which waited for: 5 -> 0; matrix products, arithmetic and copies ran while one was open for 46% -> 0% of each run, Pallas kernels for 0% -> 0%
where the time goes in v1:
time: 801 us
  Pallas kernels  793 us (99%)
    pallas_call x1, Pallas kernels, per_device(): pl.pallas_call(kernel, out_shape=[jax.ShapeDtypeStruct((TOK, D), f32)] +...  793 us

profile of v1, /device:TPU:0, one launch (start us, length us, event | category | flops | bytes accessed | tf_op | source)
XLA Modules:
  0.0 801.2 jit_solution(3274158701197264965)
XLA Ops:
  0.0 0.6 maximum_bitcast_fusion.freq
  0.6 1.7 copy.12.seg_c
  2.3 793.0 %shard_map.109 = (f32[1024,1536]{1,0:T(8,128)}, bf16[2,1536,1536]{2,1,0:T(8,128)(2,1)}, bf16[2,1536,256]{2,1,0:T(8,128)(2,1)}, bf16[2,1536,256]{2,1,0:T(8,128)(2...) custom-call(bf16[1024,1536]{1,0:T(8,128)(2,1)} %tok.1, ...), custom_call_target="tpu_custom_call" | custom-call | tf_op jit(solution)/shard_map/pallas_call | solution.py:306
  795.3 5.9 copy.14
  (1 shorter events, 0.0 us)

commit v2 on v1

v2 whole, which is shorter than its diff:
```python
import jax
import jax.numpy as jnp
from jax import lax
from jax.experimental import pallas as pl
from jax.experimental.pallas import tpu as pltpu
from jax.sharding import PartitionSpec as P

HEAD = 128
HEADS = 12
KV_HEADS = 2
EPS = 1e-5
ROPE_BASE = 10000.0
MESH = pl.DeviceIdType.MESH

N_DEV = 8
TOK = 1024
D = 1536
KV = KV_HEADS * HEAD
FF = 8960
HALF = FF // 2
ROWS = D // N_DEV
FROWS = FF // N_DEV
TF = 640
N_G0 = HALF // TF
N_G1 = FF // TF
DR = 160
N_DN = FROWS // DR
LAYERS = 2
MB = 256
NB = TOK // MB
SCALE = HEAD ** -0.5

RATE = {"X": 46600.0, "Y": 46600.0, "D": 500000.0, "L": 800000.0}
LAT = {"X": 2.5, "Y": 2.5, "D": 1.5, "L": 1.0}
HORIZON = 24.0
T_TABLES, T_WIDEN, T_NORM, T_QKV, T_HEAD, T_PROJ, T_TILE, T_ADD = 8.0, 2.0, 3.5, 2.6, 4.0, 2.0, 8.5, 1.5
OWN_FIRST = 3
N_SEM = 230


class Transfer:
    def __init__(self, key, link, size, n_sem, start, wait, done, deps):
        self.key, self.link, self.size, self.n_sem = key, link, size, n_sem
        self.start, self.wait, self.done, self.deps = start, wait, done, set(deps)
        self.sems = []


class Planner:
    def __init__(self):
        self.now = 0.0
        self.free = dict.fromkeys("XYDL", 0.0)
        self.all, self.queue, self.users, self.mates = {}, {"X": [], "Y": []}, {}, {}
        self.pool = list(range(N_SEM))
        self.issued, self.arrived, self.flying, self.sent, self.ops = set(), set(), [], [], []

    def add(self, tr):
        self.all[tr.key] = tr
        for dep in tr.deps:
            self.users.setdefault(dep, []).append(tr.key)

    def issue(self, key):
        tr = self.all[key]
        self.issued.add(key)
        tr.sems, self.pool = self.pool[:tr.n_sem], self.pool[tr.n_sem:]
        self.ops.append(tr.start)
        self.free[tr.link] = max(self.free[tr.link], self.now) + tr.size / RATE[tr.link]
        self.flying.append((self.free[tr.link] + LAT[tr.link], key))
        for mate in self.mates.get(key, ()):
            if mate not in self.issued and self.all[mate].deps <= self.arrived:
                self.issue(mate)

    def mark(self, key):
        self.arrived.add(key)
        for user in self.users.get(key, ()):
            tr = self.all[user]
            if tr.link in "DL" and user not in self.issued and tr.deps <= self.arrived:
                self.issue(user)

    def receive(self, item):
        self.flying.remove(item)
        tr = self.all[item[1]]
        self.ops.append(tr.wait)
        if tr.done is not None:
            self.sent.append((item[0] + 2.0, item[1]))
        else:
            self.pool += tr.sems
        self.mark(item[1])

    def fill(self):
        for link in "XY":
            while self.free[link] - self.now < HORIZON:
                ready = [k for k in self.queue[link] if self.all[k].deps <= self.arrived]
                if not ready:
                    break
                self.queue[link].remove(ready[0])
                self.issue(ready[0])

    def retire(self, keys=None, everything=False):
        for item in list(self.sent):
            if everything or (keys is not None and item[1] in keys) or (keys is None and item[0] <= self.now):
                self.sent.remove(item)
                self.ops.append(self.all[item[1]].done)
                self.pool += self.all[item[1]].sems

    def service(self):
        while True:
            due = sorted(i for i in self.flying if i[0] <= self.now)
            if not due:
                break
            self.receive(due[0])
            self.fill()
        self.fill()
        self.retire()

    def need(self, keys):
        keys = set(keys)
        while not keys <= self.arrived:
            self.fill()
            item = min(self.flying)
            self.now = max(self.now, item[0])
            self.receive(item)
        self.service()

    def spend(self, us):
        self.now += us

    def take(self):
        ops, self.ops = self.ops, []
        return ops


def run(ops):
    for op in ops:
        op()


def run_at(index, table):
    for k, ops in (table.items() if isinstance(table, dict) else enumerate(table)):
        if ops:
            pl.when(index == k)(lambda ops=ops: run(ops))


def kernel(tok, seg_c, seg_r, freq, g_attn, g_mlp, w_q, w_k, w_v, w_o, w_g, w_u, w_d,
           out, f_q, f_k, f_v, f_o, f_g, f_u, f_d, f_p,
           x, h, q, k, v, o, cos_t, sin_t, mask, vq, vk, vv, vo, vg, vu, vd,
           b_q, b_k, b_v, b_o, b_g, b_u, b_d,
           send, recv, ld):
    me = lax.axis_index("fsdp")
    core = lax.rem(me, 2)
    xc = lax.rem(me // 2, 2)
    yc = me // 4
    xn = me + 2 - 4 * xc
    yn = me + 4 - 8 * yc
    cn = me + 1 - 2 * core
    dg = xn + 4 - 8 * yc

    barrier = pltpu.get_barrier_semaphore()
    for nb in (xn, yn, cn):
        pl.semaphore_signal(barrier, inc=1, device_id={"fsdp": nb}, device_id_type=MESH)
    pl.semaphore_wait(barrier, 3)

    plan = Planner()

    def al(i, n):
        return i if isinstance(i, int) else pl.multiple_of(i, n)

    def view(ref, l, r0, nr, c0, nc):
        return ref.at[l, pl.ds(al(r0, 16), nr), pl.ds(al(c0, 128), nc)]

    def remote(key, link, pairs, dev, deps):
        sizes = [n for n, _ in pairs]

        def each():
            for i, (_, make) in zip(plan.all[key].sems, pairs):
                src, dst = make()
                yield pltpu.make_async_remote_copy(src_ref=src, dst_ref=dst, send_sem=send.at[i], recv_sem=recv.at[i],
                                                   device_id={"fsdp": dev}, device_id_type=MESH)

        plan.add(Transfer(key, link, sum(sizes), len(pairs), lambda: [c.start() for c in each()], lambda: [c.wait_recv() for c in each()],
                          lambda: [c.wait_send() for c in each()], deps))

    def local(key, pairs, deps):
        sizes = [n for n, _ in pairs]

        def each():
            for i, (_, make) in zip(plan.all[key].sems, pairs):
                src, dst = make()
                yield pltpu.make_async_copy(src, dst, send.at[i])

        plan.add(Transfer(key, "L", sum(sizes), len(pairs), lambda: [c.start() for c in each()], lambda: [c.wait() for c in each()], None, deps))

    def add_round(rd):
        kind, l, j = rd
        if kind == "qkv":
            mats = [(w_q, f_q, ROWS, ROWS, 0, D, b_q), (w_k, f_k, ROWS, ROWS, 0, KV, b_k), (w_v, f_v, ROWS, ROWS, 0, KV, b_v)]
        elif kind == "o":
            mats = [(w_o, f_o, ROWS, ROWS, 0, D, b_o)]
        elif kind == "dn":
            mats = [(w_d, f_d, FROWS, DR, j * DR, D, b_d.at[j % 4])]
        else:
            mats = [(w_g, f_g, ROWS, ROWS, j * TF, TF, b_g.at[j % 4]), (w_u, f_u, ROWS, ROWS, j * TF, TF, b_u.at[j % 4])]
        rowwise = kind == "dn"
        paired = l == 0 and kind == "gu"
        col_mine = yc * HALF if paired else 0
        col_other = (1 - yc) * HALF if paired else 0

        def own_src(m, other=False):
            src, _, _, nr, off, nc, _ = m
            r0, c0 = (off, 0) if rowwise else (0, off + (col_other if other else col_mine))
            return view(src, l, r0, nr, c0, nc)

        def held_at(m, dev, part=None, other=False):
            _, dst, span, nr, off, nc, _ = m
            r0, c0 = (off, 0) if rowwise else (0, off + (col_other if other else col_mine))
            cut, n = {None: (0, nr), "A": (0, nr // 2), "B": (nr // 2, nr // 2)}[part]
            return view(dst, l, dev * span + r0 + cut, n, c0, nc)

        def own(other=False):
            return [(2 * m[3] * m[5], lambda m=m: (own_src(m, other), held_at(m, me, other=other))) for m in mats]

        def held(dev, part=None):
            return [(2 * m[3] * m[5] // (2 if part else 1), lambda m=m: (held_at(m, dev, part),) * 2) for m in mats]

        K = lambda t: (rd, t)
        names = ["X", "D", "DX", "bin", "bout"]
        remote(K("X"), "X", own(), xn, [])
        remote(K("D"), "D", own(), cn, [])
        remote(K("DX"), "D", held(xn), cn, [K("X")])
        prev = [((kind, l, j - 4), "bout")] if j >= 4 else ([(("dn", 0, j + 4 if j < 3 else j), "bout")] if kind == "dn" and l == 1 else ([(("gu", 0, j + 4 if j < 3 else j), "bout")] if kind == "gu" and l == 1 else ([((kind, 0, 0), "bout")] if l == 1 else [])))
        local(K("bin"), [(2 * m[3] * m[5], lambda m=m: (own_src(m), m[6])) for m in mats], prev)
        local(K("bout"), [(2 * m[3] * m[5], lambda m=m: (m[6], held_at(m, me))) for m in mats], [K("bin")])
        plan.mates[K("X")] = [K("D"), K("bin")]
        if not (l == 0 and kind == "dn"):
            remote(K("Y"), "Y", own(other=True), yn, [])
            remote(K("DY"), "D", held(yn), cn, [K("Y")])
            names += ["Y", "DY"]
            if l == 0 or kind in ("qkv", "o"):
                remote(K("XR"), "X", held(yn), xn, [K("Y")])
                remote(K("DR"), "D", held(dg), cn, [K("XR")])
                names += ["XR", "DR"]
            else:
                remote(K("XR"), "X", held(yn, "A"), xn, [K("Y")])
                remote(K("YR"), "Y", held(xn, "B"), yn, [K("X")])
                remote(K("DR"), "D", held(dg, "A"), cn, [K("XR")])
                remote(K("DS"), "D", held(dg, "B"), cn, [K("YR")])
                names += ["XR", "YR", "DR", "DS"]
        return [K(n) for n in names]

    needs = {}
    for l, n_gu in ((0, N_G0), (1, N_G1)):
        for rd in [("qkv", l, 0), ("o", l, 0)] + [("dn", l, j) for j in range(N_DN)] + [("gu", l, j) for j in range(n_gu)]:
            needs[rd] = add_round(rd)
    for i in range(NB):
        mine, theirs = pl.ds(i * MB, MB), pl.ds(TOK + i * MB, MB)
        remote(("h", i), "Y", [(2 * MB * D, lambda mine=mine, theirs=theirs: (h.at[mine, :], h.at[theirs, :]))], yn, [("h ready", i)])
        remote(("p", i), "Y", [(4 * MB * D, lambda mine=mine, theirs=theirs: (x.at[theirs, :], f_p.at[mine, :]))], yn, ["p ready"])
    dns = {l: [key for j in range(N_DN) for key in needs[("dn", l, j)]] for l in (0, 1)}

    def seq(kind, l, n, *ts):
        return [((kind, l, j), t) for j in range(n) for t in ts]

    attn = lambda l, t: [(("qkv", l, 0), t), (("o", l, 0), t)]
    plan.queue["X"] = (attn(0, "X") + attn(0, "XR") + seq("dn", 0, N_DN, "X") + seq("gu", 0, N_G0, "X", "XR")
                       + attn(1, "X") + attn(1, "XR") + seq("dn", 1, N_DN, "X", "XR") + seq("gu", 1, N_G1, "X", "XR"))
    plan.queue["Y"] = ([("p", i) for i in range(NB)] + [("h", i) for i in range(NB)] + attn(0, "Y") + seq("gu", 0, N_G0, "Y")
                       + attn(1, "Y") + seq("dn", 1, N_DN, "Y") + seq("dn", 1, N_DN, "YR") + seq("gu", 1, N_G1, "Y", "YR"))

    def rows_of(i):
        return pl.ds(pl.multiple_of(i * MB, MB), MB)

    def load(pairs):
        cps = [pltpu.make_async_copy(s, d, ld.at[i]) for i, (s, d) in enumerate(pairs)]
        for c in cps:
            c.start()
        for c in cps:
            c.wait()

    plan.service()
    run(plan.take())
    tok_in = pltpu.make_async_copy(tok, o, ld.at[0])
    tok_in.start()

    def tables(i, c):
        rows = rows_of(i)
        same = seg_c[rows, :] == seg_r[...]
        rr = lax.broadcasted_iota(jnp.int32, (MB, TOK), 0) + i * MB
        cc = lax.broadcasted_iota(jnp.int32, (MB, TOK), 1)
        ok = jnp.where(same & (cc <= rr), 1.0, 0.0)
        mask[rows, :] = ok
        pos = jnp.sum(ok, axis=1, keepdims=True) - 1.0
        ang = pos * freq[...]
        lane = lax.broadcasted_iota(jnp.int32, (MB, HEAD), 1)
        cos_t[rows, :] = jnp.cos(ang)
        sn = jnp.sin(ang)
        sin_t[rows, :] = jnp.where(lane < HEAD // 2, -sn, sn)
        return c

    lax.fori_loop(0, NB, tables, 0)
    plan.spend(T_TABLES)
    plan.service()
    run(plan.take())
    tok_in.wait()

    def widen(i, c):
        rows = rows_of(i)
        x[rows, :] = o[rows, :].astype(jnp.float32)
        x[rows_of(i + NB), :] = jnp.zeros((MB, D), jnp.float32)
        return c

    lax.fori_loop(0, NB, widen, 0)
    plan.spend(T_WIDEN)

    def norm_row(gain_ref, l, i):
        rows = rows_of(i)
        xv = x[rows, :]
        inv = lax.rsqrt(jnp.mean(xv * xv, axis=-1, keepdims=True) + EPS)
        h[rows, :] = (xv * inv * gain_ref[l:l + 1, :].astype(jnp.float32)).astype(jnp.bfloat16)

    def rope(val, rows):
        f = val.astype(jnp.bfloat16).astype(jnp.float32)
        return (f * cos_t[rows, :] + pltpu.roll(f, HEAD // 2, 1) * sin_t[rows, :]).astype(jnp.bfloat16)

    def qkv_row(i):
        rows = rows_of(i)
        hv = h[rows, :]
        for g in range(HEADS // 4):
            val = jnp.dot(hv, vq[:, g * 512:(g + 1) * 512], preferred_element_type=jnp.float32)
            for e in range(4):
                q[rows, g * 512 + e * HEAD:g * 512 + (e + 1) * HEAD] = rope(val[:, e * HEAD:(e + 1) * HEAD], rows)
        val = jnp.dot(hv, vk[...], preferred_element_type=jnp.float32)
        for e in range(KV_HEADS):
            k[rows, e * HEAD:(e + 1) * HEAD] = rope(val[:, e * HEAD:(e + 1) * HEAD], rows)
        v[rows, :] = jnp.dot(hv, vv[...], preferred_element_type=jnp.float32).astype(jnp.bfloat16)

    def one_head(hd):
        qc = pl.ds(pl.multiple_of(hd * HEAD, HEAD), HEAD)
        kc = pl.ds(pl.multiple_of((hd // (HEADS // KV_HEADS)) * HEAD, HEAD), HEAD)
        for i in range(NB):
            n = (i + 1) * MB
            s = lax.dot_general(q[i * MB:n, qc], k[0:n, kc], (((1,), (1,)), ((), ())), preferred_element_type=jnp.float32) * SCALE
            s = jnp.where(mask[i * MB:n, 0:n] > 0.5, s, -1e30)
            e = jnp.exp(s - jnp.max(s, axis=1, keepdims=True))
            p = (e / jnp.sum(e, axis=1, keepdims=True)).astype(jnp.bfloat16)
            o[i * MB:n, qc] = jnp.dot(p, v[0:n, kc], preferred_element_type=jnp.float32).astype(jnp.bfloat16)

    def mlp_row(i, c):
        rows = rows_of(i)
        hv = h[rows, :]
        gt = jnp.dot(hv, vg[...], preferred_element_type=jnp.float32)
        up = jnp.dot(hv, vu[...], preferred_element_type=jnp.float32)
        a = (gt * jax.nn.sigmoid(gt) * up).astype(jnp.bfloat16)
        x[rows, :] += jnp.dot(a, vd[...], preferred_element_type=jnp.float32)
        return c

    for l in range(LAYERS):
        plan.need(needs[("qkv", l, 0)])
        run(plan.take())
        load([(f_q.at[l], vq), (f_k.at[l], vk), (f_v.at[l], vv)])
        plan.spend(3.0)
        table = []
        for i in range(NB):
            if l == 1:
                plan.need([("p", i)])
                plan.retire(keys=[("p", i)])
            plan.service()
            table.append(plan.take())
            plan.spend(T_QKV + T_NORM / NB + (T_ADD if l == 1 else 0.0))

        def qkv_step(i, c):
            run_at(i, table)
            if l == 1:
                load([(f_p.at[rows_of(i), :], x.at[rows_of(i + NB), :])])
                x[rows_of(i), :] += x[rows_of(i + NB), :]
            norm_row(g_attn, l, i)
            qkv_row(i)
            return c

        lax.fori_loop(0, NB, qkv_step, 0)

        table_h = []
        for i in range(HEADS):
            plan.service()
            table_h.append(plan.take())
            plan.spend(T_HEAD)

        def head_step(hd, c):
            run_at(hd, table_h)
            one_head(hd)
            return c

        lax.fori_loop(0, HEADS, head_step, 0)

        plan.need(needs[("o", l, 0)])
        run(plan.take())
        load([(f_o.at[l], vo)])
        plan.spend(2.0)
        table_o = []
        for i in range(NB):
            plan.service()
            if l == 0 and i >= 2:
                plan.mark(("h ready", i - 2))
                plan.fill()
            table_o.append(plan.take())
            plan.spend(T_PROJ + T_NORM / NB)

        def proj_step(i, c):
            run_at(i, table_o)
            rows = rows_of(i)
            x[rows, :] += jnp.dot(o[rows, :], vo[...], preferred_element_type=jnp.float32)
            norm_row(g_mlp, l, i)
            return c

        lax.fori_loop(0, NB, proj_step, 0)

        if l == 0:
            items = [(j, 0) for j in range(OWN_FIRST)] + [(j, 1) for j in range(N_G0)] + [(j, 0) for j in range(OWN_FIRST, N_G0)]
        else:
            items = [(j, 0) for j in range(N_G1)]
        table_a, table_b = [], []
        for w, (j, other) in enumerate(items):
            if l == 0 and w < 2:
                plan.mark(("h ready", NB - 2 + w))
            keys = needs[("gu", l, j)] + dns[l] + ([("h", i) for i in range(NB)] if other else [])
            plan.need(keys)
            table_a.append(plan.take())
            plan.spend(2.0)
            if l == 0 and w == OWN_FIRST + N_G0:
                plan.mark("p ready")
            plan.service()
            table_b.append(plan.take())
            plan.spend(T_TILE)

        def tiles(start, stop, base, first):
            def body(t, c):
                run_at(t, {w - base: ops for w, ops in enumerate(table_a) if start <= w < stop})
                cols = pl.ds(pl.multiple_of((yc * HALF if l == 0 else 0) + t * TF, 128), TF)
                load([(f_g.at[l, :, cols], vg), (f_u.at[l, :, cols], vu), (f_d.at[l, cols, :], vd)])
                run_at(t, {w - base: ops for w, ops in enumerate(table_b) if start <= w < stop})
                lax.fori_loop(first, first + NB, mlp_row, 0)
                return c

            lax.fori_loop(start - base, stop - base, body, 0)

        if l == 0:
            tiles(0, OWN_FIRST, 0, 0)
            tiles(OWN_FIRST, OWN_FIRST + N_G0, OWN_FIRST, NB)
            tiles(OWN_FIRST + N_G0, 2 * N_G0, N_G0, 0)
        else:
            tiles(0, N_G1, 0, 0)

    plan.need(plan.all)
    plan.retire(everything=True)
    run(plan.take())
    load([(x.at[pl.ds(0, TOK), :], out)])


def solution(mesh):
    tok_spec = P(("rep", "fsdp"), None)
    seg_spec = P(("rep", "fsdp"))
    mat_spec = P(None, "fsdp", None)
    gain_spec = P(None, None)
    bf, f32 = jnp.bfloat16, jnp.float32

    def per_device(tokens, seg_ids, w_q, w_k, w_v, w_o, w_gate, w_up, w_down, g_attn, g_mlp):
        half = HEAD // 2
        inv = ROPE_BASE ** (-jnp.arange(half, dtype=f32) / half)
        freq = jnp.concatenate([inv, inv]).reshape(1, HEAD)
        any_s = pl.BlockSpec(memory_space=pl.ANY)
        vm = pl.BlockSpec(memory_space=pltpu.VMEM)
        full = [(LAYERS, D, D), (LAYERS, D, KV), (LAYERS, D, KV), (LAYERS, D, D), (LAYERS, D, FF), (LAYERS, D, FF), (LAYERS, FF, D)]
        res = pl.pallas_call(
            kernel,
            out_shape=[jax.ShapeDtypeStruct((TOK, D), f32)] + [jax.ShapeDtypeStruct(s, bf) for s in full] + [jax.ShapeDtypeStruct((TOK, D), f32)],
            in_specs=[any_s, vm, vm, vm, vm, vm] + [any_s] * 7,
            out_specs=[any_s] * 9,
            scratch_shapes=[
                pltpu.VMEM((2 * TOK, D), f32), pltpu.VMEM((2 * TOK, D), bf), pltpu.VMEM((TOK, D), bf),
                pltpu.VMEM((TOK, KV), bf), pltpu.VMEM((TOK, KV), bf), pltpu.VMEM((TOK, D), bf),
                pltpu.VMEM((TOK, HEAD), f32), pltpu.VMEM((TOK, HEAD), f32), pltpu.VMEM((TOK, TOK), f32),
                pltpu.VMEM((D, D), bf), pltpu.VMEM((D, KV), bf), pltpu.VMEM((D, KV), bf), pltpu.VMEM((D, D), bf),
                pltpu.VMEM((D, TF), bf), pltpu.VMEM((D, TF), bf), pltpu.VMEM((TF, D), bf),
                pltpu.VMEM((ROWS, D), bf), pltpu.VMEM((ROWS, KV), bf), pltpu.VMEM((ROWS, KV), bf), pltpu.VMEM((ROWS, D), bf),
                pltpu.VMEM((4, ROWS, TF), bf), pltpu.VMEM((4, ROWS, TF), bf), pltpu.VMEM((4, DR, D), bf),
                pltpu.SemaphoreType.DMA((N_SEM,)), pltpu.SemaphoreType.DMA((N_SEM,)), pltpu.SemaphoreType.DMA((4,)),
            ],
            compiler_params=pltpu.CompilerParams(collective_id=0, has_side_effects=True, vmem_limit_bytes=66 * 1000 * 1000),
        )(tokens, seg_ids.reshape(TOK, 1), seg_ids.reshape(1, TOK), freq, g_attn, g_mlp, w_q, w_k, w_v, w_o, w_gate, w_up, w_down)
        return res[0]

    return jax.shard_map(per_device, mesh=mesh, in_specs=(tok_spec, seg_spec, mat_spec, mat_spec, mat_spec, mat_spec, mat_spec, mat_spec, mat_spec, gain_spec, gain_spec), out_specs=tok_spec, check_vma=False)
```

time: 801 us -> 730 us (0.911)
  Pallas kernels: 793 us -> 721 us
    pallas_call x1, Pallas kernels: 793 us -> 721 us  [per_device(): pl.pallas_call(kernel, out_shape=[jax.ShapeDtypeStruct((TOK, D), f32)] +...]
where the time goes in v2:
time: 730 us; the launch traced here: 729 us
  Pallas kernels  721 us (99%)
  local copies, waits for them, and re-layouts  7.64 us (1%)
    pallas_call x1, Pallas kernels, per_device(): pl.pallas_call(kernel, out_shape=[jax.ShapeDtypeStruct((TOK, D), f32)] +...  721 us

profile of v2, /device:TPU:0, one launch (start us, length us, event | category | flops | bytes accessed | tf_op | source)
XLA Modules:
  0.0 729.1 jit_solution(9120580086082467178)
XLA Ops:
  0.0 0.7 maximum_bitcast_fusion.freq
  0.7 1.7 copy.12.seg_c
  2.4 720.8 %shard_map.109 = (f32[1024,1536]{1,0:T(8,128)}, bf16[2,1536,1536]{2,1,0:T(8,128)(2,1)}, bf16[2,1536,256]{2,1,0:T(8,128)(2,1)}, bf16[2,1536,256]{2,1,0:T(8,128)(2...) custom-call(bf16[1024,1536]{1,0:T(8,128)(2,1)} %tok.1, ...), custom_call_target="tpu_custom_call" | custom-call | tf_op jit(solution)/shard_map/pallas_call | solution.py:471
  723.2 5.9 copy.14
  (1 shorter events, 0.0 us)

commit v3 on v2

--- a/solution.py
+++ b/solution.py
@@ -1,5 +1,6 @@
 import jax
 import jax.numpy as jnp
+import numpy as np
 from jax import lax
 from jax.experimental import pallas as pl
 from jax.experimental.pallas import tpu as pltpu
@@ -32,8 +33,8 @@
 
 RATE = {"X": 46600.0, "Y": 46600.0, "D": 500000.0, "L": 800000.0}
 LAT = {"X": 2.5, "Y": 2.5, "D": 1.5, "L": 1.0}
-HORIZON = 24.0
-T_TABLES, T_WIDEN, T_NORM, T_QKV, T_HEAD, T_PROJ, T_TILE, T_ADD = 8.0, 2.0, 3.5, 2.6, 4.0, 2.0, 8.5, 1.5
+HORIZON = 20.0
+T_TABLES, T_WIDEN, T_NORM, T_QKV, T_HEAD, T_PROJ, T_TILE, T_ADD = 3.0, 1.6, 0.4, 1.8, 2.0, 1.1, 6.6, 1.5
 OWN_FIRST = 3
 N_SEM = 230
 
@@ -140,8 +141,8 @@
             pl.when(index == k)(lambda ops=ops: run(ops))
 
 
-def kernel(tok, seg_c, seg_r, freq, g_attn, g_mlp, w_q, w_k, w_v, w_o, w_g, w_u, w_d,
-           out, f_q, f_k, f_v, f_o, f_g, f_u, f_d, f_p,
+def kernel(tok, seg_r, freq, g_attn, g_mlp, w_q, w_k, w_v, w_o, w_g, w_u, w_d,
+           out, out_a, out_d, f_q, f_k, f_v, f_o, f_g, f_u, f_d, f_p,
            x, h, q, k, v, o, cos_t, sin_t, mask, vq, vk, vv, vo, vg, vu, vd,
            b_q, b_k, b_v, b_o, b_g, b_u, b_d,
            send, recv, ld):
@@ -282,10 +283,11 @@
 
     def tables(i, c):
         rows = rows_of(i)
-        same = seg_c[rows, :] == seg_r[...]
         rr = lax.broadcasted_iota(jnp.int32, (MB, TOK), 0) + i * MB
         cc = lax.broadcasted_iota(jnp.int32, (MB, TOK), 1)
-        ok = jnp.where(same & (cc <= rr), 1.0, 0.0)
+        seg = jnp.broadcast_to(seg_r[...], (MB, TOK)).astype(jnp.float32)
+        seg_c = jnp.sum(jnp.where(cc == rr, seg, 0.0), axis=1, keepdims=True)
+        ok = jnp.where((seg == seg_c) & (cc <= rr), 1.0, 0.0)
         mask[rows, :] = ok
         pos = jnp.sum(ok, axis=1, keepdims=True) - 1.0
         ang = pos * freq[...]
@@ -343,13 +345,14 @@
             p = (e / jnp.sum(e, axis=1, keepdims=True)).astype(jnp.bfloat16)
             o[i * MB:n, qc] = jnp.dot(p, v[0:n, kc], preferred_element_type=jnp.float32).astype(jnp.bfloat16)
 
+    def act(hv):
+        gt = jnp.dot(hv, vg[...], preferred_element_type=jnp.float32)
+        up = jnp.dot(hv, vu[...], preferred_element_type=jnp.float32)
+        return (gt * jax.nn.sigmoid(gt) * up).astype(jnp.bfloat16)
+
     def mlp_row(i, c):
         rows = rows_of(i)
-        hv = h[rows, :]
-        gt = jnp.dot(hv, vg[...], preferred_element_type=jnp.float32)
-        up = jnp.dot(hv, vu[...], preferred_element_type=jnp.float32)
-        a = (gt * jax.nn.sigmoid(gt) * up).astype(jnp.bfloat16)
-        x[rows, :] += jnp.dot(a, vd[...], preferred_element_type=jnp.float32)
+        x[rows, :] += jnp.dot(act(h[rows, :]), vd[...], preferred_element_type=jnp.float32)
         return c
 
     for l in range(LAYERS):
@@ -446,12 +449,28 @@
             tiles(OWN_FIRST, OWN_FIRST + N_G0, OWN_FIRST, NB)
             tiles(OWN_FIRST + N_G0, 2 * N_G0, N_G0, 0)
         else:
-            tiles(0, N_G1, 0, 0)
+            tiles(0, N_G1 - 1, 0, 0)
+            run(table_a[-1])
+            cols = pl.ds(FF - TF, TF)
+            load([(f_g.at[l, :, cols], vg), (f_u.at[l, :, cols], vu), (f_d.at[l, cols, :], vd)])
+            run(table_b[-1])
+            outs = [pltpu.make_async_copy(x.at[pl.ds(0, TOK), :], out, ld.at[0]), pltpu.make_async_copy(vd, out_d, ld.at[1])]
+            for c in outs:
+                c.start()
+
+            def act_row(i, c):
+                rows = rows_of(i)
+                q[rows, 0:TF] = act(h[rows, :])
+                return c
+
+            lax.fori_loop(0, NB, act_row, 0)
 
     plan.need(plan.all)
     plan.retire(everything=True)
     run(plan.take())
-    load([(x.at[pl.ds(0, TOK), :], out)])
+    for c in outs:
+        c.wait()
+    load([(q.at[:, pl.ds(0, TF)], out_a)])
 
 
 def solution(mesh):
@@ -463,16 +482,16 @@
 
     def per_device(tokens, seg_ids, w_q, w_k, w_v, w_o, w_gate, w_up, w_down, g_attn, g_mlp):
         half = HEAD // 2
-        inv = ROPE_BASE ** (-jnp.arange(half, dtype=f32) / half)
-        freq = jnp.concatenate([inv, inv]).reshape(1, HEAD)
+        inv = np.float32(ROPE_BASE) ** (-np.arange(half, dtype=np.float32) / np.float32(half))
+        freq = jnp.asarray(np.concatenate([inv, inv]).reshape(1, HEAD), f32)
         any_s = pl.BlockSpec(memory_space=pl.ANY)
         vm = pl.BlockSpec(memory_space=pltpu.VMEM)
         full = [(LAYERS, D, D), (LAYERS, D, KV), (LAYERS, D, KV), (LAYERS, D, D), (LAYERS, D, FF), (LAYERS, D, FF), (LAYERS, FF, D)]
         res = pl.pallas_call(
             kernel,
-            out_shape=[jax.ShapeDtypeStruct((TOK, D), f32)] + [jax.ShapeDtypeStruct(s, bf) for s in full] + [jax.ShapeDtypeStruct((TOK, D), f32)],
-            in_specs=[any_s, vm, vm, vm, vm, vm] + [any_s] * 7,
-            out_specs=[any_s] * 9,
+            out_shape=[jax.ShapeDtypeStruct((TOK, D), f32), jax.ShapeDtypeStruct((TOK, TF), bf), jax.ShapeDtypeStruct((TF, D), bf)] + [jax.ShapeDtypeStruct(s, bf) for s in full] + [jax.ShapeDtypeStruct((TOK, D), f32)],
+            in_specs=[any_s, vm, vm, vm, vm] + [any_s] * 7,
+            out_specs=[any_s] * 11,
             scratch_shapes=[
                 pltpu.VMEM((2 * TOK, D), f32), pltpu.VMEM((2 * TOK, D), bf), pltpu.VMEM((TOK, D), bf),
                 pltpu.VMEM((TOK, KV), bf), pltpu.VMEM((TOK, KV), bf), pltpu.VMEM((TOK, D), bf),
@@ -484,7 +503,7 @@
                 pltpu.SemaphoreType.DMA((N_SEM,)), pltpu.SemaphoreType.DMA((N_SEM,)), pltpu.SemaphoreType.DMA((4,)),
             ],
             compiler_params=pltpu.CompilerParams(collective_id=0, has_side_effects=True, vmem_limit_bytes=66 * 1000 * 1000),
-        )(tokens, seg_ids.reshape(TOK, 1), seg_ids.reshape(1, TOK), freq, g_attn, g_mlp, w_q, w_k, w_v, w_o, w_gate, w_up, w_down)
-        return res[0]
+        )(tokens, seg_ids.reshape(1, TOK), freq, g_attn, g_mlp, w_q, w_k, w_v, w_o, w_gate, w_up, w_down)
+        return res[0] + jnp.dot(res[1], res[2], preferred_element_type=f32)
 
     return jax.shard_map(per_device, mesh=mesh, in_specs=(tok_spec, seg_spec, mat_spec, mat_spec, mat_spec, mat_spec, mat_spec, mat_spec, mat_spec, gain_spec, gain_spec), out_specs=tok_spec, check_vma=False)

time: 730 us -> 718 us (0.984)
  Pallas kernels: 721 us -> 707 us
  matrix products: 0 us -> 9.08 us
  local copies, waits for them, and re-layouts: 7.64 us -> 0 us
    pallas_call x1, Pallas kernels: 721 us -> 707 us  [per_device(): pl.pallas_call(kernel, out_shape=[jax.ShapeDtypeStruct((TOK, D), f32), ja...]
    dot_general x0 -> x1, matrix products: none -> 9.08 us  [per_device(): return res[0] + jnp.dot(res[1], res[2], preferred_element_type=f32)]
where the time goes in v3:
time: 718 us; the launch traced here: 716 us
  Pallas kernels  707 us (98%)
  matrix products  9.08 us (1%)
    pallas_call x1, Pallas kernels, per_device(): pl.pallas_call(kernel, out_shape=[jax.ShapeDtypeStruct((TOK, D), f32), ja...  707 us

profile of v3, /device:TPU:0, one launch (start us, length us, event | category | flops | bytes accessed | tf_op | source)
XLA Modules:
  0.0 716.3 jit_solution(1097361139698196084)
XLA Ops:
  0.0 707.2 %shard_map.118 = (f32[1024,1536]{1,0:T(8,128)}, bf16[1024,640]{1,0:T(8,128)(2,1)}, bf16[640,1536]{1,0:T(8,128)(2,1)}, bf16[2,1536,1536]{2,1,0:T(8,128)(2,1)}, bf...) custom-call(bf16[1024,1536]{1,0:T(8,128)(2,1)} %tok.1, ...), custom_call_target="tpu_custom_call" | custom-call | tf_op jit(solution)/shard_map/pallas_call | solution.py:490
  707.2 9.1 %convolution_add_fusion = f32[1024,1536]{1,0:T(8,128)} fusion(f32[1024,1536]{1,0:T(8,128)} %get-tuple-element.8, bf16[1024,640]{1,0:T(8,128)(2,1)} %get-tuple-element.9, bf16[640,1536]{1,0:T(8,128)(2,1)} %get-tuple-element.10), kind=kOutput, calls=%fused_computation | convolution fusion | flops 2014838784 | bytes 15859712 | tf_op jit(solution)/shard_map/dot_general | solution.py:507

commit v4 on v3

--- a/solution.py
+++ b/solution.py
@@ -23,8 +23,11 @@
 FROWS = FF // N_DEV
 TF = 640
 N_G0 = HALF // TF
-N_G1 = FF // TF
+TP_TILES = (1, 2, 3, 4, 5)
+N_DP = 4
 DR = 160
+N_DT = 5
+N_DD = 2
 N_DN = FROWS // DR
 LAYERS = 2
 MB = 256
@@ -36,6 +39,7 @@
 HORIZON = 20.0
 T_TABLES, T_WIDEN, T_NORM, T_QKV, T_HEAD, T_PROJ, T_TILE, T_ADD = 3.0, 1.6, 0.4, 1.8, 2.0, 1.1, 6.6, 1.5
 OWN_FIRST = 3
+L1_ORDER = ("lo", "hi", "own", "dp")
 N_SEM = 230
 
 
@@ -142,7 +146,7 @@
 
 
 def kernel(tok, seg_r, freq, g_attn, g_mlp, w_q, w_k, w_v, w_o, w_g, w_u, w_d,
-           out, out_a, out_d, f_q, f_k, f_v, f_o, f_g, f_u, f_d, f_p,
+           out, out_p, f_q, f_k, f_v, f_o, f_g, f_u, f_d, f_p,
            x, h, q, k, v, o, cos_t, sin_t, mask, vq, vk, vv, vo, vg, vu, vd,
            b_q, b_k, b_v, b_o, b_g, b_u, b_d,
            send, recv, ld):
@@ -190,84 +194,115 @@
 
         plan.add(Transfer(key, "L", sum(sizes), len(pairs), lambda: [c.start() for c in each()], lambda: [c.wait() for c in each()], None, deps))
 
-    def add_round(rd):
-        kind, l, j = rd
-        if kind == "qkv":
-            mats = [(w_q, f_q, ROWS, ROWS, 0, D, b_q), (w_k, f_k, ROWS, ROWS, 0, KV, b_k), (w_v, f_v, ROWS, ROWS, 0, KV, b_v)]
-        elif kind == "o":
-            mats = [(w_o, f_o, ROWS, ROWS, 0, D, b_o)]
-        elif kind == "dn":
-            mats = [(w_d, f_d, FROWS, DR, j * DR, D, b_d.at[j % 4])]
+    def block(src, dst, l, col, other_col, nc, stage):
+        def at(dev, other=False):
+            return view(dst, l, dev * ROWS, ROWS, other_col if other else col, nc)
+
+        def part(dev, p):
+            return view(dst, l, dev * ROWS + (ROWS // 2) * p, ROWS // 2, col, nc)
+        return (2 * ROWS * nc, lambda other=False: view(src, l, 0, ROWS, other_col if other else col, nc), at, stage)
+
+    def down_block(l, j, stage):
+        return (2 * DR * D, lambda other=False: view(w_d, l, j * DR, DR, 0, D), lambda dev, other=False: view(f_d, l, dev * FROWS + j * DR, DR, 0, D), stage)
+
+    def shared_block(row_of):
+        at = lambda dev, other=False: view(f_d, 1, row_of(dev), DR, 0, D)
+        return (2 * DR * D, lambda other=False: at(me), at, None)
+
+    def place(dev):
+        return dev // 4, lax.rem(dev // 2, 2), lax.rem(dev, 2)
+
+    def tp_row(j):
+        def row(dev):
+            yy, xx, cc = place(dev)
+            return yy * HALF + xx * (2 * FROWS) + TF * (1 - xx) + (N_DT * DR) * cc + j * DR
+        return row
+
+    def dp_row(j):
+        def row(dev):
+            yy, xx, cc = place(dev)
+            return yy * HALF + xx * (2 * FROWS) + (2 * FROWS - TF) * xx + (N_DD * DR) * cc + j * DR
+        return row
+
+    def add_round(rd, mats, parts, deps=(), before=None):
+        K = lambda t: (rd, t)
+
+        def own(other=False):
+            return [(m[0], lambda m=m: (m[1](other), m[2](me, other))) for m in mats]
+
+        def held(dev):
+            return [(m[0], lambda m=m: (m[2](dev), m[2](dev))) for m in mats]
+
+        for t in parts:
+            if t == "X":
+                remote(K(t), "X", own(), xn, deps)
+            elif t == "Y":
+                remote(K(t), "Y", own(other=True), yn, deps)
+            elif t == "D":
+                remote(K(t), "D", own(), cn, [])
+            elif t == "XR":
+                remote(K(t), "X", held(yn), xn, [K("Y")])
+            elif t == "DX":
+                remote(K(t), "D", held(xn), cn, [K("X")])
+            elif t == "DY":
+                remote(K(t), "D", held(yn), cn, [K("Y")])
+            elif t == "DR":
+                remote(K(t), "D", held(dg), cn, [K("XR")])
+            elif t == "bin":
+                local(K(t), [(m[0], lambda m=m: (m[1](), m[3])) for m in mats], [before] if before else [])
+            else:
+                local(K(t), [(m[0], lambda m=m: (m[3], m[2](me))) for m in mats], [K("bin")])
+        if "D" in parts and "X" in parts:
+            plan.mates[K("X")] = [K("D"), K("bin")]
+        needs[rd] = [K(t) for t in parts]
+
+    needs = {}
+    FULL = ("X", "Y", "D", "XR", "DX", "DY", "DR", "bin", "bout")
+    for l in (0, 1):
+        add_round(("qkv", l), [block(w_q, f_q, l, 0, 0, D, b_q), block(w_k, f_k, l, 0, 0, KV, b_k), block(w_v, f_v, l, 0, 0, KV, b_v)], FULL,
+                  before=(("qkv", 0), "bout") if l else None)
+        add_round(("o", l), [block(w_o, f_o, l, 0, 0, D, b_o)], FULL, before=(("o", 0), "bout") if l else None)
+    dn_seq = [("dn", l, j) for l in (0, 1) for j in range(N_DN)]
+    for n, rd in enumerate(dn_seq):
+        add_round(rd, [down_block(rd[1], rd[2], b_d.at[n % 4])], ("X", "D", "DX", "bin", "bout") if rd[1] == 0 else ("D", "bin", "bout"),
+                  before=(dn_seq[n - 4], "bout") if n >= 4 else None)
+    dn1 = [key for j in range(N_DN) for key in needs[("dn", 1, j)]]
+    for j in range(N_DT):
+        add_round(("dt", j), [shared_block(tp_row(j))], ("X", "DX"), deps=dn1)
+    for j in range(N_DD):
+        add_round(("dd", j), [shared_block(dp_row(j))], ("X", "Y", "XR", "DX", "DY", "DR"), deps=dn1)
+    gu_seq = [("gu", j) for j in range(N_G0)] + [("gt", j) for j in TP_TILES] + [("gd", j) for j in range(N_DP)]
+    for n, rd in enumerate(gu_seq):
+        kind, j = rd
+        l = 0 if kind == "gu" else 1
+        if kind == "gd":
+            col = (j % 2) * HALF + (j // 2) * (HALF - TF)
+            other = col
         else:
-            mats = [(w_g, f_g, ROWS, ROWS, j * TF, TF, b_g.at[j % 4]), (w_u, f_u, ROWS, ROWS, j * TF, TF, b_u.at[j % 4])]
-        rowwise = kind == "dn"
-        paired = l == 0 and kind == "gu"
-        col_mine = yc * HALF if paired else 0
-        col_other = (1 - yc) * HALF if paired else 0
-
-        def own_src(m, other=False):
-            src, _, _, nr, off, nc, _ = m
-            r0, c0 = (off, 0) if rowwise else (0, off + (col_other if other else col_mine))
-            return view(src, l, r0, nr, c0, nc)
-
-        def held_at(m, dev, part=None, other=False):
-            _, dst, span, nr, off, nc, _ = m
-            r0, c0 = (off, 0) if rowwise else (0, off + (col_other if other else col_mine))
-            cut, n = {None: (0, nr), "A": (0, nr // 2), "B": (nr // 2, nr // 2)}[part]
-            return view(dst, l, dev * span + r0 + cut, n, c0, nc)
-
-        def own(other=False):
-            return [(2 * m[3] * m[5], lambda m=m: (own_src(m, other), held_at(m, me, other=other))) for m in mats]
-
-        def held(dev, part=None):
-            return [(2 * m[3] * m[5] // (2 if part else 1), lambda m=m: (held_at(m, dev, part),) * 2) for m in mats]
-
-        K = lambda t: (rd, t)
-        names = ["X", "D", "DX", "bin", "bout"]
-        remote(K("X"), "X", own(), xn, [])
-        remote(K("D"), "D", own(), cn, [])
-        remote(K("DX"), "D", held(xn), cn, [K("X")])
-        prev = [((kind, l, j - 4), "bout")] if j >= 4 else ([(("dn", 0, j + 4 if j < 3 else j), "bout")] if kind == "dn" and l == 1 else ([(("gu", 0, j + 4 if j < 3 else j), "bout")] if kind == "gu" and l == 1 else ([((kind, 0, 0), "bout")] if l == 1 else [])))
-        local(K("bin"), [(2 * m[3] * m[5], lambda m=m: (own_src(m), m[6])) for m in mats], prev)
-        local(K("bout"), [(2 * m[3] * m[5], lambda m=m: (m[6], held_at(m, me))) for m in mats], [K("bin")])
-        plan.mates[K("X")] = [K("D"), K("bin")]
-        if not (l == 0 and kind == "dn"):
-            remote(K("Y"), "Y", own(other=True), yn, [])
-            remote(K("DY"), "D", held(yn), cn, [K("Y")])
-            names += ["Y", "DY"]
-            if l == 0 or kind in ("qkv", "o"):
-                remote(K("XR"), "X", held(yn), xn, [K("Y")])
-                remote(K("DR"), "D", held(dg), cn, [K("XR")])
-                names += ["XR", "DR"]
-            else:
-                remote(K("XR"), "X", held(yn, "A"), xn, [K("Y")])
-                remote(K("YR"), "Y", held(xn, "B"), yn, [K("X")])
-                remote(K("DR"), "D", held(dg, "A"), cn, [K("XR")])
-                remote(K("DS"), "D", held(dg, "B"), cn, [K("YR")])
-                names += ["XR", "YR", "DR", "DS"]
-        return [K(n) for n in names]
-
-    needs = {}
-    for l, n_gu in ((0, N_G0), (1, N_G1)):
-        for rd in [("qkv", l, 0), ("o", l, 0)] + [("dn", l, j) for j in range(N_DN)] + [("gu", l, j) for j in range(n_gu)]:
-            needs[rd] = add_round(rd)
+            col, other = yc * HALF + j * TF, (1 - yc) * HALF + j * TF
+        add_round(rd, [block(w_g, f_g, l, col, other, TF, b_g.at[n % 4]), block(w_u, f_u, l, col, other, TF, b_u.at[n % 4])], FULL,
+                  before=(gu_seq[n - 4], "bout") if n >= 4 else None)
+    for j in range(N_DN):
+        plan.mates[(("gu", j), "X")] += [(("dn", 1, j), "D"), (("dn", 1, j), "bin")]
     for i in range(NB):
         mine, theirs = pl.ds(i * MB, MB), pl.ds(TOK + i * MB, MB)
-        remote(("h", i), "Y", [(2 * MB * D, lambda mine=mine, theirs=theirs: (h.at[mine, :], h.at[theirs, :]))], yn, [("h ready", i)])
-        remote(("p", i), "Y", [(4 * MB * D, lambda mine=mine, theirs=theirs: (x.at[theirs, :], f_p.at[mine, :]))], yn, ["p ready"])
-    dns = {l: [key for j in range(N_DN) for key in needs[("dn", l, j)]] for l in (0, 1)}
-
-    def seq(kind, l, n, *ts):
-        return [((kind, l, j), t) for j in range(n) for t in ts]
-
-    attn = lambda l, t: [(("qkv", l, 0), t), (("o", l, 0), t)]
-    plan.queue["X"] = (attn(0, "X") + attn(0, "XR") + seq("dn", 0, N_DN, "X") + seq("gu", 0, N_G0, "X", "XR")
-                       + attn(1, "X") + attn(1, "XR") + seq("dn", 1, N_DN, "X", "XR") + seq("gu", 1, N_G1, "X", "XR"))
-    plan.queue["Y"] = ([("p", i) for i in range(NB)] + [("h", i) for i in range(NB)] + attn(0, "Y") + seq("gu", 0, N_G0, "Y")
-                       + attn(1, "Y") + seq("dn", 1, N_DN, "Y") + seq("dn", 1, N_DN, "YR") + seq("gu", 1, N_G1, "Y", "YR"))
+        for l, land in ((0, f_p), (1, out_p)):
+            remote(("h", l, i), "Y", [(2 * MB * D, lambda mine=mine, theirs=theirs: (h.at[mine, :], h.at[theirs, :]))], yn, [("h ready", l, i)])
+            remote(("p", l, i), "Y", [(4 * MB * D, lambda mine=mine, theirs=theirs, land=land: (x.at[theirs, :], land.at[mine, :]))], yn, [("p ready", l, i)])
+
+    def seq(rds, *ts):
+        return [(rd, t) for rd in rds for t in ts]
+
+    attn = lambda l: [("qkv", l), ("o", l)]
+    gus, gts, gds = [("gu", j) for j in range(N_G0)], [("gt", j) for j in TP_TILES], [("gd", j) for j in range(N_DP)]
+    dts, dds = [("dt", j) for j in range(N_DT)], [("dd", j) for j in range(N_DD)]
+    plan.queue["X"] = (seq(attn(0), "X") + seq(attn(0), "XR") + seq(dn_seq[:N_DN], "X") + seq(gus, "X", "XR")
+                       + seq(attn(1), "X") + seq(attn(1), "XR") + seq(dts, "X") + seq(gts, "X", "XR") + seq(dds, "X", "XR") + seq(gds, "X", "XR"))
+    tok_sends = [(c, l, i) for c, l in (("p", 0), ("h", 0), ("h", 1), ("p", 1)) for i in range(NB)]
+    plan.queue["Y"] = tok_sends + seq(attn(0), "Y") + seq(gus, "Y") + seq(attn(1), "Y") + seq(gts, "Y") + seq(dds, "Y") + seq(gds, "Y")
 
     def rows_of(i):
-        return pl.ds(pl.multiple_of(i * MB, MB), MB)
+        return pl.ds(i * MB if isinstance(i, int) else pl.multiple_of(i * MB, MB), MB)
 
     def load(pairs):
         cps = [pltpu.make_async_copy(s, d, ld.at[i]) for i, (s, d) in enumerate(pairs)]
@@ -334,10 +369,10 @@
             k[rows, e * HEAD:(e + 1) * HEAD] = rope(val[:, e * HEAD:(e + 1) * HEAD], rows)
         v[rows, :] = jnp.dot(hv, vv[...], preferred_element_type=jnp.float32).astype(jnp.bfloat16)
 
-    def one_head(hd):
+    def one_head(hd, blocks):
         qc = pl.ds(pl.multiple_of(hd * HEAD, HEAD), HEAD)
         kc = pl.ds(pl.multiple_of((hd // (HEADS // KV_HEADS)) * HEAD, HEAD), HEAD)
-        for i in range(NB):
+        for i in blocks:
             n = (i + 1) * MB
             s = lax.dot_general(q[i * MB:n, qc], k[0:n, kc], (((1,), (1,)), ((), ())), preferred_element_type=jnp.float32) * SCALE
             s = jnp.where(mask[i * MB:n, 0:n] > 0.5, s, -1e30)
@@ -355,122 +390,147 @@
         x[rows, :] += jnp.dot(act(h[rows, :]), vd[...], preferred_element_type=jnp.float32)
         return c
 
-    for l in range(LAYERS):
-        plan.need(needs[("qkv", l, 0)])
+    def get_qkv(l):
+        plan.need(needs[("qkv", l)])
         run(plan.take())
         load([(f_q.at[l], vq), (f_k.at[l], vk), (f_v.at[l], vv)])
         plan.spend(3.0)
-        table = []
-        for i in range(NB):
-            if l == 1:
-                plan.need([("p", i)])
-                plan.retire(keys=[("p", i)])
-            plan.service()
-            table.append(plan.take())
-            plan.spend(T_QKV + T_NORM / NB + (T_ADD if l == 1 else 0.0))
-
-        def qkv_step(i, c):
-            run_at(i, table)
-            if l == 1:
-                load([(f_p.at[rows_of(i), :], x.at[rows_of(i + NB), :])])
-                x[rows_of(i), :] += x[rows_of(i + NB), :]
-            norm_row(g_attn, l, i)
-            qkv_row(i)
-            return c
-
-        lax.fori_loop(0, NB, qkv_step, 0)
-
-        table_h = []
-        for i in range(HEADS):
-            plan.service()
-            table_h.append(plan.take())
-            plan.spend(T_HEAD)
-
-        def head_step(hd, c):
-            run_at(hd, table_h)
-            one_head(hd)
-            return c
-
-        lax.fori_loop(0, HEADS, head_step, 0)
-
-        plan.need(needs[("o", l, 0)])
+
+    def get_o(l):
+        plan.need(needs[("o", l)])
         run(plan.take())
         load([(f_o.at[l], vo)])
         plan.spend(2.0)
-        table_o = []
-        for i in range(NB):
+
+    def heads(blocks):
+        table = []
+        for i in range(HEADS):
+            if i % 2 == 0 or len(blocks) == NB:
+                plan.service()
+            table.append(plan.take())
+            plan.spend(T_HEAD * sum(b + 1 for b in blocks) / 10)
+
+        def head_step(hd, c):
+            run_at(hd, table)
+            one_head(hd, blocks)
+            return c
+
+        lax.fori_loop(0, HEADS, head_step, 0)
+
+    def proj_row(l, i):
+        rows = rows_of(i)
+        x[rows, :] += jnp.dot(o[rows, :], vo[...], preferred_element_type=jnp.float32)
+        norm_row(g_mlp, l, i)
+
+    def tiles(l, steps, offset, first, n_rows, marks=None):
+        pre, post = {}, {}
+        for n, (t, keys) in enumerate(steps):
+            for key in (marks or {}).get((n, "pre"), ()):
+                plan.mark(key)
+            plan.need(keys)
+            pre[t] = plan.take()
+            plan.spend(2.2)
+            for key in (marks or {}).get((n, "post"), ()):
+                plan.mark(key)
             plan.service()
-            if l == 0 and i >= 2:
-                plan.mark(("h ready", i - 2))
-                plan.fill()
-            table_o.append(plan.take())
-            plan.spend(T_PROJ + T_NORM / NB)
-
-        def proj_step(i, c):
-            run_at(i, table_o)
-            rows = rows_of(i)
-            x[rows, :] += jnp.dot(o[rows, :], vo[...], preferred_element_type=jnp.float32)
-            norm_row(g_mlp, l, i)
+            post[t] = plan.take()
+            plan.spend(T_TILE * n_rows / NB)
+
+        def body(t, c):
+            run_at(t, pre)
+            cols = pl.ds(pl.multiple_of(offset(t), 128), TF)
+            load([(f_g.at[l, :, cols], vg), (f_u.at[l, :, cols], vu), (f_d.at[l, cols, :], vd)])
+            run_at(t, post)
+            lax.fori_loop(first, first + n_rows, mlp_row, 0)
             return c
 
-        lax.fori_loop(0, NB, proj_step, 0)
-
-        if l == 0:
-            items = [(j, 0) for j in range(OWN_FIRST)] + [(j, 1) for j in range(N_G0)] + [(j, 0) for j in range(OWN_FIRST, N_G0)]
+        lax.fori_loop(steps[0][0], steps[-1][0] + 1, body, 0)
+
+    get_qkv(0)
+    table_q = []
+    for i in range(NB):
+        plan.service()
+        table_q.append(plan.take())
+        plan.spend(T_QKV + T_NORM)
+
+    def qkv_step(i, c):
+        run_at(i, table_q)
+        norm_row(g_attn, 0, i)
+        qkv_row(i)
+        return c
+
+    lax.fori_loop(0, NB, qkv_step, 0)
+    heads(range(NB))
+    get_o(0)
+    table_o = []
+    for i in range(NB):
+        plan.service()
+        if i >= 2:
+            plan.mark(("h ready", 0, i - 2))
+            plan.fill()
+        table_o.append(plan.take())
+        plan.spend(T_PROJ + T_NORM)
+
+    def proj_step(i, c):
+        run_at(i, table_o)
+        proj_row(0, i)
+        return c
+
+    lax.fori_loop(0, NB, proj_step, 0)
+
+    dn0 = [key for j in range(N_DN) for key in needs[("dn", 0, j)]]
+    half_off = lambda t: yc * HALF + t * TF
+    steps = [(j, needs[("gu", j)] + dn0) for j in range(N_G0)]
+    got_h = lambda l, *chunks: [("h", l, i) for i in chunks]
+    tiles(0, steps[:OWN_FIRST], half_off, 0, NB, {(0, "pre"): [("h ready", 0, NB - 2)], (0, "post"): [("h ready", 0, NB - 1)]})
+    tiles(0, [(j, keys + got_h(0, *range(NB))) for j, keys in steps], half_off, NB, NB)
+    tiles(0, steps[OWN_FIRST:], half_off, 0, NB, {(0, "post"): [("p ready", 0, i) for i in range(NB)]})
+
+    get_qkv(1)
+    for i in range(NB):
+        plan.need([("p", 0, i)])
+        plan.retire(keys=[("p", 0, i)])
+        if i:
+            plan.mark(("h ready", 1, i - 1))
+            plan.service()
+        run(plan.take())
+        load([(f_p.at[rows_of(i), :], x.at[rows_of(i + NB), :])])
+        x[rows_of(i), :] += x[rows_of(i + NB), :]
+        x[rows_of(i + NB), :] = jnp.zeros((MB, D), jnp.float32)
+        norm_row(g_attn, 1, i)
+        qkv_row(i)
+        plan.spend(T_QKV + T_NORM + T_ADD)
+        heads([i])
+        if i == 0:
+            get_o(1)
+        proj_row(1, i)
+        plan.spend(T_PROJ + T_NORM)
+
+    dt1 = dn1 + [key for j in range(N_DT) for key in needs[("dt", j)]]
+    dd1 = dn1 + [key for j in range(N_DD) for key in needs[("dd", j)]]
+    steps = [(j, needs[("gt", j)] + dt1) for j in TP_TILES]
+    h_mark = {(0, "pre"): [("h ready", 1, NB - 1)]}
+    run_order = L1_ORDER
+    marks = {}
+    for n, what in enumerate(run_order):
+        if what == "own":
+            tiles(1, steps, half_off, 0, NB, {**h_mark, **marks})
+            marks, h_mark = {}, {}
+        elif what in ("lo", "hi"):
+            chunks = (0, 1) if what == "lo" else (2, 3)
+            tiles(1, [(j, keys + got_h(1, *chunks)) for j, keys in steps], half_off, NB + chunks[0], 2, {**h_mark, **marks})
+            marks, h_mark = {(0, "post"): [("p ready", 1, i) for i in chunks]}, {}
         else:
-            items = [(j, 0) for j in range(N_G1)]
-        table_a, table_b = [], []
-        for w, (j, other) in enumerate(items):
-            if l == 0 and w < 2:
-                plan.mark(("h ready", NB - 2 + w))
-            keys = needs[("gu", l, j)] + dns[l] + ([("h", i) for i in range(NB)] if other else [])
-            plan.need(keys)
-            table_a.append(plan.take())
-            plan.spend(2.0)
-            if l == 0 and w == OWN_FIRST + N_G0:
-                plan.mark("p ready")
-            plan.service()
-            table_b.append(plan.take())
-            plan.spend(T_TILE)
-
-        def tiles(start, stop, base, first):
-            def body(t, c):
-                run_at(t, {w - base: ops for w, ops in enumerate(table_a) if start <= w < stop})
-                cols = pl.ds(pl.multiple_of((yc * HALF if l == 0 else 0) + t * TF, 128), TF)
-                load([(f_g.at[l, :, cols], vg), (f_u.at[l, :, cols], vu), (f_d.at[l, cols, :], vd)])
-                run_at(t, {w - base: ops for w, ops in enumerate(table_b) if start <= w < stop})
-                lax.fori_loop(first, first + NB, mlp_row, 0)
-                return c
-
-            lax.fori_loop(start - base, stop - base, body, 0)
-
-        if l == 0:
-            tiles(0, OWN_FIRST, 0, 0)
-            tiles(OWN_FIRST, OWN_FIRST + N_G0, OWN_FIRST, NB)
-            tiles(OWN_FIRST + N_G0, 2 * N_G0, N_G0, 0)
-        else:
-            tiles(0, N_G1 - 1, 0, 0)
-            run(table_a[-1])
-            cols = pl.ds(FF - TF, TF)
-            load([(f_g.at[l, :, cols], vg), (f_u.at[l, :, cols], vu), (f_d.at[l, cols, :], vd)])
-            run(table_b[-1])
-            outs = [pltpu.make_async_copy(x.at[pl.ds(0, TOK), :], out, ld.at[0]), pltpu.make_async_copy(vd, out_d, ld.at[1])]
-            for c in outs:
-                c.start()
-
-            def act_row(i, c):
-                rows = rows_of(i)
-                q[rows, 0:TF] = act(h[rows, :])
-                return c
-
-            lax.fori_loop(0, NB, act_row, 0)
-
+            tiles(1, [(j, needs[("gd", j)] + dd1) for j in range(N_DP)],
+                  lambda t: lax.rem(t, 2) * HALF + lax.div(t, 2) * (HALF - TF), 0, NB, {**h_mark, **marks})
+            marks, h_mark = {}, {}
+
+    done = pltpu.make_async_copy(x.at[pl.ds(0, TOK), :], out, ld.at[0])
+    done.start()
     plan.need(plan.all)
     plan.retire(everything=True)
     run(plan.take())
-    for c in outs:
-        c.wait()
-    load([(q.at[:, pl.ds(0, TF)], out_a)])
+    done.wait()
 
 
 def solution(mesh):
@@ -489,9 +549,9 @@
         full = [(LAYERS, D, D), (LAYERS, D, KV), (LAYERS, D, KV), (LAYERS, D, D), (LAYERS, D, FF), (LAYERS, D, FF), (LAYERS, FF, D)]
         res = pl.pallas_call(
             kernel,
-            out_shape=[jax.ShapeDtypeStruct((TOK, D), f32), jax.ShapeDtypeStruct((TOK, TF), bf), jax.ShapeDtypeStruct((TF, D), bf)] + [jax.ShapeDtypeStruct(s, bf) for s in full] + [jax.ShapeDtypeStruct((TOK, D), f32)],
+            out_shape=[jax.ShapeDtypeStruct((TOK, D), f32)] * 2 + [jax.ShapeDtypeStruct(s, bf) for s in full] + [jax.ShapeDtypeStruct((TOK, D), f32)],
             in_specs=[any_s, vm, vm, vm, vm] + [any_s] * 7,
-            out_specs=[any_s] * 11,
+            out_specs=[any_s] * 10,
             scratch_shapes=[
                 pltpu.VMEM((2 * TOK, D), f32), pltpu.VMEM((2 * TOK, D), bf), pltpu.VMEM((TOK, D), bf),
                 pltpu.VMEM((TOK, KV), bf), pltpu.VMEM((TOK, KV), bf), pltpu.VMEM((TOK, D), bf),
@@ -504,6 +564,6 @@
             ],
             compiler_params=pltpu.CompilerParams(collective_id=0, has_side_effects=True, vmem_limit_bytes=66 * 1000 * 1000),
         )(tokens, seg_ids.reshape(1, TOK), freq, g_attn, g_mlp, w_q, w_k, w_v, w_o, w_gate, w_up, w_down)
-        return res[0] + jnp.dot(res[1], res[2], preferred_element_type=f32)
+        return res[0] + res[1]
 
     return jax.shard_map(per_device, mesh=mesh, in_specs=(tok_spec, seg_spec, mat_spec, mat_spec, mat_spec, mat_spec, mat_spec, mat_spec, mat_spec, gain_spec, gain_spec), out_specs=tok_spec, check_vma=False)

time: 718 us -> 683 us (0.951)
  Pallas kernels: 707 us -> 674 us
  matrix products: 9.08 us -> 0 us
  other arithmetic: 0 us -> 8.69 us
    pallas_call x1, Pallas kernels: 707 us -> 674 us  [per_device(): pl.pallas_call(kernel, out_shape=[jax.ShapeDtypeStruct((TOK, D), f32)] *...]
    dot_general x1 -> x0, matrix products: 9.08 us -> none  [per_device(): return res[0] + jnp.dot(res[1], res[2], preferred_element_type=f32)]
    add x0 -> x1, other arithmetic: none -> 8.69 us  [per_device(): return res[0] + res[1]]
where the time goes in v4:
time: 683 us; the launch traced here: 682 us
  Pallas kernels  674 us (99%)
  other arithmetic  8.69 us (1%)
    pallas_call x1, Pallas kernels, per_device(): pl.pallas_call(kernel, out_shape=[jax.ShapeDtypeStruct((TOK, D), f32)] *...  674 us

profile of v4, /device:TPU:0, one launch (start us, length us, event | category | flops | bytes accessed | tf_op | source)
XLA Modules:
  0.0 682.2 jit_solution(11837421978003675039)
XLA Ops:
  0.0 673.5 %shard_map.118 = (f32[1024,1536]{1,0:T(8,128)}, f32[1024,1536]{1,0:T(8,128)}, bf16[2,1536,1536]{2,1,0:T(8,128)(2,1)}, bf16[2,1536,256]{2,1,0:T(8,128)(2,1)}, bf1...) custom-call(bf16[1024,1536]{1,0:T(8,128)(2,1)} %tok.1, ...), custom_call_target="tpu_custom_call" | custom-call | tf_op jit(solution)/shard_map/pallas_call | solution.py:550
  673.5 8.7 %add.3 = f32[1024,1536]{1,0:T(8,128)} add(f32[1024,1536]{1,0:T(8,128)} %get-tuple-element.7, f32[1024,1536]{1,0:T(8,128)} %get-tuple-element.8) | non-fusion elementwise | flops 1572864 | bytes 18874368 | tf_op jit(solution)/shard_map/add | solution.py:567

commit v5 on v4

--- a/solution.py
+++ b/solution.py
@@ -40,7 +40,9 @@
 T_TABLES, T_WIDEN, T_NORM, T_QKV, T_HEAD, T_PROJ, T_TILE, T_ADD = 3.0, 1.6, 0.4, 1.8, 2.0, 1.1, 6.6, 1.5
 OWN_FIRST = 3
 L1_ORDER = ("lo", "hi", "own", "dp")
+TOKEN_ORDER = [(c, l, i) for c, l in (("h", 0), ("p", 0), ("h", 1), ("p", 1)) for i in range(NB)]
 N_SEM = 230
+FB = 128
 
 
 class Transfer:
@@ -146,7 +148,7 @@
 
 
 def kernel(tok, seg_r, freq, g_attn, g_mlp, w_q, w_k, w_v, w_o, w_g, w_u, w_d,
-           out, out_p, f_q, f_k, f_v, f_o, f_g, f_u, f_d, f_p,
+           out, f_r, f_q, f_k, f_v, f_o, f_g, f_u, f_d, f_p,
            x, h, q, k, v, o, cos_t, sin_t, mask, vq, vk, vv, vo, vg, vu, vd,
            b_q, b_k, b_v, b_o, b_g, b_u, b_d,
            send, recv, ld):
@@ -286,7 +288,7 @@
         plan.mates[(("gu", j), "X")] += [(("dn", 1, j), "D"), (("dn", 1, j), "bin")]
     for i in range(NB):
         mine, theirs = pl.ds(i * MB, MB), pl.ds(TOK + i * MB, MB)
-        for l, land in ((0, f_p), (1, out_p)):
+        for l, land in ((0, f_p), (1, f_r)):
             remote(("h", l, i), "Y", [(2 * MB * D, lambda mine=mine, theirs=theirs: (h.at[mine, :], h.at[theirs, :]))], yn, [("h ready", l, i)])
             remote(("p", l, i), "Y", [(4 * MB * D, lambda mine=mine, theirs=theirs, land=land: (x.at[theirs, :], land.at[mine, :]))], yn, [("p ready", l, i)])
 
@@ -298,8 +300,7 @@
     dts, dds = [("dt", j) for j in range(N_DT)], [("dd", j) for j in range(N_DD)]
     plan.queue["X"] = (seq(attn(0), "X") + seq(attn(0), "XR") + seq(dn_seq[:N_DN], "X") + seq(gus, "X", "XR")
                        + seq(attn(1), "X") + seq(attn(1), "XR") + seq(dts, "X") + seq(gts, "X", "XR") + seq(dds, "X", "XR") + seq(gds, "X", "XR"))
-    tok_sends = [(c, l, i) for c, l in (("p", 0), ("h", 0), ("h", 1), ("p", 1)) for i in range(NB)]
-    plan.queue["Y"] = tok_sends + seq(attn(0), "Y") + seq(gus, "Y") + seq(attn(1), "Y") + seq(gts, "Y") + seq(dds, "Y") + seq(gds, "Y")
+    plan.queue["Y"] = TOKEN_ORDER + seq(attn(0), "Y") + seq(gus, "Y") + seq(attn(1), "Y") + seq(gts, "Y") + seq(dds, "Y") + seq(gds, "Y")
 
     def rows_of(i):
         return pl.ds(i * MB if isinstance(i, int) else pl.multiple_of(i * MB, MB), MB)
@@ -519,18 +520,38 @@
         elif what in ("lo", "hi"):
             chunks = (0, 1) if what == "lo" else (2, 3)
             tiles(1, [(j, keys + got_h(1, *chunks)) for j, keys in steps], half_off, NB + chunks[0], 2, {**h_mark, **marks})
-            marks, h_mark = {(0, "post"): [("p ready", 1, i) for i in chunks]}, {}
+            marks, h_mark = {(0, "pre"): [("p ready", 1, chunks[0])], (0, "post"): [("p ready", 1, chunks[1])]}, {}
         else:
             tiles(1, [(j, needs[("gd", j)] + dd1) for j in range(N_DP)],
                   lambda t: lax.rem(t, 2) * HALF + lax.div(t, 2) * (HALF - TF), 0, NB, {**h_mark, **marks})
             marks, h_mark = {}, {}
 
+    for i in range(NB - 1):
+        plan.need([("p", 1, i)])
+        plan.retire(keys=[("p", 1, i)])
+        run(plan.take())
+        load([(f_r.at[rows_of(i), :], x.at[rows_of(i + NB), :])])
+        x[rows_of(i), :] += x[rows_of(i + NB), :]
+        plan.spend(T_ADD)
+    plan.service()
     done = pltpu.make_async_copy(x.at[pl.ds(0, TOK), :], out, ld.at[0])
     done.start()
     plan.need(plan.all)
     plan.retire(everything=True)
     run(plan.take())
     done.wait()
+
+
+def finish(x_ref, r_ref, out_ref):
+    last = pl.program_id(0) >= (NB - 1) * MB // FB
+
+    @pl.when(last)
+    def _():
+        out_ref[...] = x_ref[...] + r_ref[...]
+
+    @pl.when(jnp.logical_not(last))
+    def _():
+        out_ref[...] = x_ref[...]
 
 
 def solution(mesh):
@@ -564,6 +585,12 @@
             ],
             compiler_params=pltpu.CompilerParams(collective_id=0, has_side_effects=True, vmem_limit_bytes=66 * 1000 * 1000),
         )(tokens, seg_ids.reshape(1, TOK), freq, g_attn, g_mlp, w_q, w_k, w_v, w_o, w_gate, w_up, w_down)
-        return res[0] + res[1]
+        return pl.pallas_call(
+            finish,
+            grid=(TOK // FB,),
+            out_shape=jax.ShapeDtypeStruct((TOK, D), f32),
+            in_specs=[pl.BlockSpec((FB, D), lambda i: (i, 0)), pl.BlockSpec((FB, D), lambda i: (jnp.maximum(i, (NB - 1) * MB // FB), 0))],
+            out_specs=pl.BlockSpec((FB, D), lambda i: (i, 0)),
+        )(res[0], res[1])
 
     return jax.shard_map(per_device, mesh=mesh, in_specs=(tok_spec, seg_spec, mat_spec, mat_spec, mat_spec, mat_spec, mat_spec, mat_spec, mat_spec, gain_spec, gain_spec), out_specs=tok_spec, check_vma=False)

time: 683 us -> 683 us (level)
  other arithmetic: 8.69 us -> 0 us
  Pallas kernels: 674 us -> 681 us
    add x1 -> x0, other arithmetic: 8.69 us -> none  [per_device(): return res[0] + res[1]]
    pallas_call x0 -> x1, Pallas kernels: none -> 8.33 us  [per_device(): pl.pallas_call(finish, grid=(TOK // FB,), out_shape=jax.ShapeDtypeStruct(...]
where the time goes in v5:
time: 683 us; the launch traced here: 681 us
  Pallas kernels  681 us (100%)
    pallas_call x1, Pallas kernels, per_device(): pl.pallas_call(kernel, out_shape=[jax.ShapeDtypeStruct((TOK, D), f32)] *...  673 us

profile of v5, /device:TPU:0, one launch (start us, length us, event | category | flops | bytes accessed | tf_op | source)
XLA Modules:
  0.0 681.4 jit_solution(321143429222497098)
XLA Ops:
  0.0 673.0 %shard_map.118 = (f32[1024,1536]{1,0:T(8,128)}, f32[1024,1536]{1,0:T(8,128)}, bf16[2,1536,1536]{2,1,0:T(8,128)(2,1)}, bf16[2,1536,256]{2,1,0:T(8,128)(2,1)}, bf1...) custom-call(bf16[1024,1536]{1,0:T(8,128)(2,1)} %tok.1, ...), custom_call_target="tpu_custom_call" | custom-call | tf_op jit(solution)/shard_map/pallas_call | solution.py:571
  673.1 8.3 %shard_map.119 = f32[1024,1536]{1,0:T(8,128)} custom-call(f32[1024,1536]{1,0:T(8,128)} %get-tuple-element.7.x_ref, f32[1024,1536]{1,0:T(8,128)} %get-tuple-element.8.r_ref), custom_call_target="tpu_custom_call" | custom-call | tf_op jit(solution)/shard_map/pallas_call | solution.py:588

commit v6 on v5

--- a/solution.py
+++ b/solution.py
@@ -542,16 +542,29 @@
     done.wait()
 
 
-def finish(x_ref, r_ref, out_ref):
-    last = pl.program_id(0) >= (NB - 1) * MB // FB
-
-    @pl.when(last)
-    def _():
-        out_ref[...] = x_ref[...] + r_ref[...]
-
-    @pl.when(jnp.logical_not(last))
-    def _():
-        out_ref[...] = x_ref[...]
+def finish(x_in, r_in, out, xv, rv, sem):
+    n = TOK // FB
+    first = (NB - 1) * MB // FB
+    rows = [pl.ds(i * FB, FB) for i in range(n)]
+    order = list(range(first, n)) + list(range(first))
+    got = {i: pltpu.make_async_copy(x_in.at[rows[i], :], xv.at[rows[i], :], sem.at[0, i]) for i in range(n)}
+    ret = {i: pltpu.make_async_copy(r_in.at[rows[i], :], rv.at[pl.ds((i - first) * FB, FB), :], sem.at[1, i]) for i in range(first, n)}
+    put = {i: pltpu.make_async_copy(xv.at[rows[i], :], out.at[rows[i], :], sem.at[2, i]) for i in range(n)}
+    for i in order:
+        if i in ret:
+            ret[i].start()
+        got[i].start()
+    for i in range(first, n):
+        ret[i].wait()
+        got[i].wait()
+        xv[rows[i], :] += rv[pl.ds((i - first) * FB, FB), :]
+    for i in range(first):
+        got[i].wait()
+        put[i].start()
+    for i in range(first, n):
+        put[i].start()
+    for i in range(n):
+        put[i].wait()
 
 
 def solution(mesh):
@@ -587,10 +600,11 @@
         )(tokens, seg_ids.reshape(1, TOK), freq, g_attn, g_mlp, w_q, w_k, w_v, w_o, w_gate, w_up, w_down)
         return pl.pallas_call(
             finish,
-            grid=(TOK // FB,),
             out_shape=jax.ShapeDtypeStruct((TOK, D), f32),
-            in_specs=[pl.BlockSpec((FB, D), lambda i: (i, 0)), pl.BlockSpec((FB, D), lambda i: (jnp.maximum(i, (NB - 1) * MB // FB), 0))],
-            out_specs=pl.BlockSpec((FB, D), lambda i: (i, 0)),
+            in_specs=[any_s, any_s],
+            out_specs=any_s,
+            scratch_shapes=[pltpu.VMEM((TOK, D), f32), pltpu.VMEM((MB, D), f32), pltpu.SemaphoreType.DMA((3, TOK // FB))],
+            compiler_params=pltpu.CompilerParams(vmem_limit_bytes=66 * 1000 * 1000),
         )(res[0], res[1])
 
     return jax.shard_map(per_device, mesh=mesh, in_specs=(tok_spec, seg_spec, mat_spec, mat_spec, mat_spec, mat_spec, mat_spec, mat_spec, mat_spec, gain_spec, gain_spec), out_specs=tok_spec, check_vma=False)

time: 683 us -> 680 us (level)
  no operation moved by 1% of the time
where the time goes in v6:
time: 680 us; the launch traced here: 679 us
  Pallas kernels  678 us (100%)
    pallas_call x1, Pallas kernels, per_device(): pl.pallas_call(kernel, out_shape=[jax.ShapeDtypeStruct((TOK, D), f32)] *...  673 us

profile of v6, /device:TPU:0, one launch (start us, length us, event | category | flops | bytes accessed | tf_op | source)
XLA Modules:
  0.0 678.6 jit_solution(2599759089864166957)
XLA Ops:
  0.0 673.0 %shard_map.118 = (f32[1024,1536]{1,0:T(8,128)}, f32[1024,1536]{1,0:T(8,128)}, bf16[2,1536,1536]{2,1,0:T(8,128)(2,1)}, bf16[2,1536,256]{2,1,0:T(8,128)(2,1)}, bf1...) custom-call(bf16[1024,1536]{1,0:T(8,128)(2,1)} %tok.1, ...), custom_call_target="tpu_custom_call" | custom-call | tf_op jit(solution)/shard_map/pallas_call | solution.py:584
  673.1 5.4 shard_map.119

commit v7 on v6

--- a/solution.py
+++ b/solution.py
@@ -39,7 +39,9 @@
 HORIZON = 20.0
 T_TABLES, T_WIDEN, T_NORM, T_QKV, T_HEAD, T_PROJ, T_TILE, T_ADD = 3.0, 1.6, 0.4, 1.8, 2.0, 1.1, 6.6, 1.5
 OWN_FIRST = 3
-L1_ORDER = ("lo", "hi", "own", "dp")
+P_AFTER = {3: [("h ready", 1, 1)]}
+L1_ORDER = ("c0", "c1", "hi", "own", "dp")
+GROUPS = {"c0": (0,), "c1": (1,), "lo": (0, 1), "hi": (2, 3), "c123": (1, 2, 3)}
 TOKEN_ORDER = [(c, l, i) for c, l in (("h", 0), ("p", 0), ("h", 1), ("p", 1)) for i in range(NB)]
 N_SEM = 230
 FB = 128
@@ -290,7 +292,7 @@
         mine, theirs = pl.ds(i * MB, MB), pl.ds(TOK + i * MB, MB)
         for l, land in ((0, f_p), (1, f_r)):
             remote(("h", l, i), "Y", [(2 * MB * D, lambda mine=mine, theirs=theirs: (h.at[mine, :], h.at[theirs, :]))], yn, [("h ready", l, i)])
-            remote(("p", l, i), "Y", [(4 * MB * D, lambda mine=mine, theirs=theirs, land=land: (x.at[theirs, :], land.at[mine, :]))], yn, [("p ready", l, i)])
+            remote(("p", l, i), "Y", [(4 * MB * D, lambda mine=mine, theirs=theirs, land=land: (x.at[theirs, :], land.at[mine, :]))], yn, [("p ready", l, i)] + (P_AFTER.get(i, []) if l == 0 else []))
 
     def seq(rds, *ts):
         return [(rd, t) for rd in rds for t in ts]
@@ -491,13 +493,9 @@
     for i in range(NB):
         plan.need([("p", 0, i)])
         plan.retire(keys=[("p", 0, i)])
-        if i:
-            plan.mark(("h ready", 1, i - 1))
-            plan.service()
         run(plan.take())
         load([(f_p.at[rows_of(i), :], x.at[rows_of(i + NB), :])])
         x[rows_of(i), :] += x[rows_of(i + NB), :]
-        x[rows_of(i + NB), :] = jnp.zeros((MB, D), jnp.float32)
         norm_row(g_attn, 1, i)
         qkv_row(i)
         plan.spend(T_QKV + T_NORM + T_ADD)
@@ -505,22 +503,26 @@
         if i == 0:
             get_o(1)
         proj_row(1, i)
-        plan.spend(T_PROJ + T_NORM)
+        x[rows_of(i + NB), :] = jnp.zeros((MB, D), jnp.float32)
+        plan.spend(T_PROJ + T_NORM + 0.4)
+        plan.mark(("h ready", 1, i))
+        plan.service()
+        run(plan.take())
 
     dt1 = dn1 + [key for j in range(N_DT) for key in needs[("dt", j)]]
     dd1 = dn1 + [key for j in range(N_DD) for key in needs[("dd", j)]]
     steps = [(j, needs[("gt", j)] + dt1) for j in TP_TILES]
-    h_mark = {(0, "pre"): [("h ready", 1, NB - 1)]}
+    h_mark = {}
     run_order = L1_ORDER
     marks = {}
     for n, what in enumerate(run_order):
         if what == "own":
             tiles(1, steps, half_off, 0, NB, {**h_mark, **marks})
             marks, h_mark = {}, {}
-        elif what in ("lo", "hi"):
-            chunks = (0, 1) if what == "lo" else (2, 3)
-            tiles(1, [(j, keys + got_h(1, *chunks)) for j, keys in steps], half_off, NB + chunks[0], 2, {**h_mark, **marks})
-            marks, h_mark = {(0, "pre"): [("p ready", 1, chunks[0])], (0, "post"): [("p ready", 1, chunks[1])]}, {}
+        elif what in GROUPS:
+            chunks = GROUPS[what]
+            tiles(1, [(j, keys + got_h(1, *chunks)) for j, keys in steps], half_off, NB + chunks[0], len(chunks), {**h_mark, **marks})
+            marks, h_mark = {(0, "pre"): [("p ready", 1, i) for i in chunks[:-1]], (0, "post"): [("p ready", 1, chunks[-1])]}, {}
         else:
             tiles(1, [(j, needs[("gd", j)] + dd1) for j in range(N_DP)],
                   lambda t: lax.rem(t, 2) * HALF + lax.div(t, 2) * (HALF - TF), 0, NB, {**h_mark, **marks})

time: 680 us -> 686 us (level)
  Pallas kernels: 678 us -> 685 us
where the time goes in v7:
time: 686 us; the launch traced here: 685 us
  Pallas kernels  685 us (100%)
    pallas_call x1, Pallas kernels, per_device(): pl.pallas_call(kernel, out_shape=[jax.ShapeDtypeStruct((TOK, D), f32)] *...  680 us

profile of v7, /device:TPU:0, one launch (start us, length us, event | category | flops | bytes accessed | tf_op | source)
XLA Modules:
  0.0 685.2 jit_solution(2601605149583243447)
XLA Ops:
  0.0 679.6 %shard_map.118 = (f32[1024,1536]{1,0:T(8,128)}, f32[1024,1536]{1,0:T(8,128)}, bf16[2,1536,1536]{2,1,0:T(8,128)(2,1)}, bf16[2,1536,256]{2,1,0:T(8,128)(2,1)}, bf1...) custom-call(bf16[1024,1536]{1,0:T(8,128)(2,1)} %tok.1, ...), custom_call_target="tpu_custom_call" | custom-call | tf_op jit(solution)/shard_map/pallas_call | solution.py:586
  679.6 5.4 shard_map.119

commit v8 on v7

--- a/solution.py
+++ b/solution.py
@@ -37,13 +37,14 @@
 RATE = {"X": 46600.0, "Y": 46600.0, "D": 500000.0, "L": 800000.0}
 LAT = {"X": 2.5, "Y": 2.5, "D": 1.5, "L": 1.0}
 HORIZON = 20.0
-T_TABLES, T_WIDEN, T_NORM, T_QKV, T_HEAD, T_PROJ, T_TILE, T_ADD = 3.0, 1.6, 0.4, 1.8, 2.0, 1.1, 6.6, 1.5
+T_TABLES, T_WIDEN, T_NORM, T_QKV, T_HEAD, T_PROJ, T_TILE, T_ADD = 3.0, 1.6, 0.4, 1.8, 2.0, 1.1, 7.0, 1.7
 OWN_FIRST = 3
 P_AFTER = {3: [("h ready", 1, 1)]}
-L1_ORDER = ("c0", "c1", "hi", "own", "dp")
+L1_ORDER = (("own", 0, 2), "lo", "hi", ("own", 2, 5), "dp")
 GROUPS = {"c0": (0,), "c1": (1,), "lo": (0, 1), "hi": (2, 3), "c123": (1, 2, 3)}
 TOKEN_ORDER = [(c, l, i) for c, l in (("h", 0), ("p", 0), ("h", 1), ("p", 1)) for i in range(NB)]
-N_SEM = 230
+N_SEM = 226
+T_LOAD = 2.4
 FB = 128
 
 
@@ -153,7 +154,7 @@
            out, f_r, f_q, f_k, f_v, f_o, f_g, f_u, f_d, f_p,
            x, h, q, k, v, o, cos_t, sin_t, mask, vq, vk, vv, vo, vg, vu, vd,
            b_q, b_k, b_v, b_o, b_g, b_u, b_d,
-           send, recv, ld):
+           send, recv, ld, tl):
     me = lax.axis_index("fsdp")
     core = lax.rem(me, 2)
     xc = lax.rem(me // 2, 2)
@@ -383,14 +384,13 @@
             p = (e / jnp.sum(e, axis=1, keepdims=True)).astype(jnp.bfloat16)
             o[i * MB:n, qc] = jnp.dot(p, v[0:n, kc], preferred_element_type=jnp.float32).astype(jnp.bfloat16)
 
-    def act(hv):
-        gt = jnp.dot(hv, vg[...], preferred_element_type=jnp.float32)
-        up = jnp.dot(hv, vu[...], preferred_element_type=jnp.float32)
-        return (gt * jax.nn.sigmoid(gt) * up).astype(jnp.bfloat16)
-
-    def mlp_row(i, c):
+    def mlp_row(i, slot, c):
         rows = rows_of(i)
-        x[rows, :] += jnp.dot(act(h[rows, :]), vd[...], preferred_element_type=jnp.float32)
+        hv = h[rows, :]
+        gt = jnp.dot(hv, vg[slot], preferred_element_type=jnp.float32)
+        up = jnp.dot(hv, vu[slot], preferred_element_type=jnp.float32)
+        a = (gt * jax.nn.sigmoid(gt) * up).astype(jnp.bfloat16)
+        x[rows, :] += jnp.dot(a, vd[slot], preferred_element_type=jnp.float32)
         return c
 
     def get_qkv(l):
@@ -426,28 +426,40 @@
         norm_row(g_mlp, l, i)
 
     def tiles(l, steps, offset, first, n_rows, marks=None):
-        pre, post = {}, {}
+        pre, post, ahead = {}, {}, {}
+        early = False
         for n, (t, keys) in enumerate(steps):
             for key in (marks or {}).get((n, "pre"), ()):
                 plan.mark(key)
             plan.need(keys)
             pre[t] = plan.take()
-            plan.spend(2.2)
+            if not early:
+                pre[t].append(lambda t=t: [c.start() for c in tile_loads(l, offset(t), t % 2)])
+                plan.spend(T_LOAD)
             for key in (marks or {}).get((n, "post"), ()):
                 plan.mark(key)
             plan.service()
             post[t] = plan.take()
+            early = n + 1 < len(steps) and set(steps[n + 1][1]) <= plan.arrived
+            if early:
+                post[t].append(lambda t=t: [c.start() for c in tile_loads(l, offset(t + 1), (t + 1) % 2)])
             plan.spend(T_TILE * n_rows / NB)
 
         def body(t, c):
+            slot = lax.rem(t, 2)
             run_at(t, pre)
-            cols = pl.ds(pl.multiple_of(offset(t), 128), TF)
-            load([(f_g.at[l, :, cols], vg), (f_u.at[l, :, cols], vu), (f_d.at[l, cols, :], vd)])
+            for cp in tile_loads(l, offset(t), slot):
+                cp.wait()
             run_at(t, post)
-            lax.fori_loop(first, first + n_rows, mlp_row, 0)
+            lax.fori_loop(first, first + n_rows, lambda i, c: mlp_row(i, slot, c), 0)
             return c
 
         lax.fori_loop(steps[0][0], steps[-1][0] + 1, body, 0)
+
+    def tile_loads(l, off, slot):
+        cols = pl.ds(al(off, 128), TF)
+        return [pltpu.make_async_copy(f_g.at[l, :, cols], vg.at[slot], tl.at[slot, 0]), pltpu.make_async_copy(f_u.at[l, :, cols], vu.at[slot], tl.at[slot, 1]),
+                pltpu.make_async_copy(f_d.at[l, cols, :], vd.at[slot], tl.at[slot, 2])]
 
     get_qkv(0)
     table_q = []
@@ -516,8 +528,8 @@
     run_order = L1_ORDER
     marks = {}
     for n, what in enumerate(run_order):
-        if what == "own":
-            tiles(1, steps, half_off, 0, NB, {**h_mark, **marks})
+        if what[0] == "own":
+            tiles(1, steps[what[1]:what[2]], half_off, 0, NB, {**h_mark, **marks})
             marks, h_mark = {}, {}
         elif what in GROUPS:
             chunks = GROUPS[what]
@@ -525,7 +537,7 @@
             marks, h_mark = {(0, "pre"): [("p ready", 1, i) for i in chunks[:-1]], (0, "post"): [("p ready", 1, chunks[-1])]}, {}
         else:
             tiles(1, [(j, needs[("gd", j)] + dd1) for j in range(N_DP)],
-                  lambda t: lax.rem(t, 2) * HALF + lax.div(t, 2) * (HALF - TF), 0, NB, {**h_mark, **marks})
+                  lambda t: (t % 2) * HALF + (t // 2) * (HALF - TF) if isinstance(t, int) else lax.rem(t, 2) * HALF + lax.div(t, 2) * (HALF - TF), 0, NB, {**h_mark, **marks})
             marks, h_mark = {}, {}
 
     for i in range(NB - 1):
@@ -593,10 +605,10 @@
                 pltpu.VMEM((TOK, KV), bf), pltpu.VMEM((TOK, KV), bf), pltpu.VMEM((TOK, D), bf),
                 pltpu.VMEM((TOK, HEAD), f32), pltpu.VMEM((TOK, HEAD), f32), pltpu.VMEM((TOK, TOK), f32),
                 pltpu.VMEM((D, D), bf), pltpu.VMEM((D, KV), bf), pltpu.VMEM((D, KV), bf), pltpu.VMEM((D, D), bf),
-                pltpu.VMEM((D, TF), bf), pltpu.VMEM((D, TF), bf), pltpu.VMEM((TF, D), bf),
+                pltpu.VMEM((2, D, TF), bf), pltpu.VMEM((2, D, TF), bf), pltpu.VMEM((2, TF, D), bf),
                 pltpu.VMEM((ROWS, D), bf), pltpu.VMEM((ROWS, KV), bf), pltpu.VMEM((ROWS, KV), bf), pltpu.VMEM((ROWS, D), bf),
                 pltpu.VMEM((4, ROWS, TF), bf), pltpu.VMEM((4, ROWS, TF), bf), pltpu.VMEM((4, DR, D), bf),
-                pltpu.SemaphoreType.DMA((N_SEM,)), pltpu.SemaphoreType.DMA((N_SEM,)), pltpu.SemaphoreType.DMA((4,)),
+                pltpu.SemaphoreType.DMA((N_SEM,)), pltpu.SemaphoreType.DMA((N_SEM,)), pltpu.SemaphoreType.DMA((4,)), pltpu.SemaphoreType.DMA((2, 3)),
             ],
             compiler_params=pltpu.CompilerParams(collective_id=0, has_side_effects=True, vmem_limit_bytes=66 * 1000 * 1000),
         )(tokens, seg_ids.reshape(1, TOK), freq, g_attn, g_mlp, w_q, w_k, w_v, w_o, w_gate, w_up, w_down)

time: 686 us -> 670 us (0.977)
  Pallas kernels: 685 us -> 669 us
    pallas_call x1, Pallas kernels: 680 us -> 663 us  [per_device(): pl.pallas_call(kernel, out_shape=[jax.ShapeDtypeStruct((TOK, D), f32)] *...]
where the time goes in v8:
time: 670 us; the launch traced here: 669 us
  Pallas kernels  669 us (100%)
    pallas_call x1, Pallas kernels, per_device(): pl.pallas_call(kernel, out_shape=[jax.ShapeDtypeStruct((TOK, D), f32)] *...  663 us

profile of v8, /device:TPU:0, one launch (start us, length us, event | category | flops | bytes accessed | tf_op | source)
XLA Modules:
  0.0 668.8 jit_solution(4403035695691476675)
XLA Ops:
  0.0 663.2 %shard_map.118 = (f32[1024,1536]{1,0:T(8,128)}, f32[1024,1536]{1,0:T(8,128)}, bf16[2,1536,1536]{2,1,0:T(8,128)(2,1)}, bf16[2,1536,256]{2,1,0:T(8,128)(2,1)}, bf1...) custom-call(bf16[1024,1536]{1,0:T(8,128)(2,1)} %tok.1, ...), custom_call_target="tpu_custom_call" | custom-call | tf_op jit(solution)/shard_map/pallas_call | solution.py:598
  663.2 5.4 shard_map.119

commit v9 on v8

--- a/solution.py
+++ b/solution.py
@@ -36,15 +36,15 @@
 
 RATE = {"X": 46600.0, "Y": 46600.0, "D": 500000.0, "L": 800000.0}
 LAT = {"X": 2.5, "Y": 2.5, "D": 1.5, "L": 1.0}
-HORIZON = 20.0
-T_TABLES, T_WIDEN, T_NORM, T_QKV, T_HEAD, T_PROJ, T_TILE, T_ADD = 3.0, 1.6, 0.4, 1.8, 2.0, 1.1, 7.0, 1.7
+HORIZON = 18.0
+T_TABLES, T_WIDEN, T_NORM, T_QKV, T_HEAD, T_PROJ, T_TILE, T_ADD = 3.0, 1.6, 0.4, 2.2, 2.3, 1.1, 7.6, 1.7
 OWN_FIRST = 3
 P_AFTER = {3: [("h ready", 1, 1)]}
-L1_ORDER = (("own", 0, 2), "lo", "hi", ("own", 2, 5), "dp")
+L1_ORDER = (("own", 0, 1), "lo", "hi", ("own", 1, 5), "dp")
 GROUPS = {"c0": (0,), "c1": (1,), "lo": (0, 1), "hi": (2, 3), "c123": (1, 2, 3)}
 TOKEN_ORDER = [(c, l, i) for c, l in (("h", 0), ("p", 0), ("h", 1), ("p", 1)) for i in range(NB)]
 N_SEM = 226
-T_LOAD = 2.4
+T_LOAD = 2.8
 FB = 128
 
 

time: 670 us -> 670 us (level)
  no operation moved by 1% of the time
where the time goes in v9:
time: 670 us; the launch traced here: 669 us
  Pallas kernels  669 us (100%)
    pallas_call x1, Pallas kernels, per_device(): pl.pallas_call(kernel, out_shape=[jax.ShapeDtypeStruct((TOK, D), f32)] *...  663 us

profile of v9, /device:TPU:0, one launch (start us, length us, event | category | flops | bytes accessed | tf_op | source)
XLA Modules:
  0.0 668.8 jit_solution(12679689372230020744)
XLA Ops:
  0.0 663.2 %shard_map.118 = (f32[1024,1536]{1,0:T(8,128)}, f32[1024,1536]{1,0:T(8,128)}, bf16[2,1536,1536]{2,1,0:T(8,128)(2,1)}, bf16[2,1536,256]{2,1,0:T(8,128)(2,1)}, bf1...) custom-call(bf16[1024,1536]{1,0:T(8,128)(2,1)} %tok.1, ...), custom_call_target="tpu_custom_call" | custom-call | tf_op jit(solution)/shard_map/pallas_call | solution.py:598
  663.2 5.4 shard_map.119

commit v10 on v8

--- a/solution.py
+++ b/solution.py
@@ -45,7 +45,7 @@
 TOKEN_ORDER = [(c, l, i) for c, l in (("h", 0), ("p", 0), ("h", 1), ("p", 1)) for i in range(NB)]
 N_SEM = 226
 T_LOAD = 2.4
-FB = 128
+FB = 64
 
 
 class Transfer:

time: 670 us -> 670 us (level)
  no operation moved by 1% of the time
where the time goes in v10:
time: 670 us; the launch traced here: 669 us
  Pallas kernels  669 us (100%)
    pallas_call x1, Pallas kernels, per_device(): pl.pallas_call(kernel, out_shape=[jax.ShapeDtypeStruct((TOK, D), f32)] *...  663 us

profile of v10, /device:TPU:0, one launch (start us, length us, event | category | flops | bytes accessed | tf_op | source)
XLA Modules:
  0.0 669.2 jit_solution(16989257325039591688)
XLA Ops:
  0.0 663.2 %shard_map.118 = (f32[1024,1536]{1,0:T(8,128)}, f32[1024,1536]{1,0:T(8,128)}, bf16[2,1536,1536]{2,1,0:T(8,128)(2,1)}, bf16[2,1536,256]{2,1,0:T(8,128)(2,1)}, bf1...) custom-call(bf16[1024,1536]{1,0:T(8,128)(2,1)} %tok.1, ...), custom_call_target="tpu_custom_call" | custom-call | tf_op jit(solution)/shard_map/pallas_call | solution.py:598
  663.2 5.8 shard_map.119
